TPU v7x, 16 devices: a whole 2x2x2 slice. The times are simulated.
16 devices in a mesh: dp: 4 (over z, y), ep: 4 (over x, core).
Axes of the slice: x: 2, y: 2, z: 2, core: 2. Of those that a mesh axis runs over, the one named last changes fastest.
Arguments:
- tokens: bfloat16 [4096, 2048], P(('dp', 'ep')), parts along dimension 0
- expert_ids: int32 [4096, 6], P(('dp', 'ep')), parts along dimension 0
- gate_vals: float32 [4096, 6], P(('dp', 'ep')), parts along dimension 0
- slots: int32 [4096, 6], P(('dp', 'ep')), parts along dimension 0
- shared_w1: bfloat16 [2048, 2816], replicated
- shared_w3: bfloat16 [2048, 2816], replicated
- shared_w2: bfloat16 [2816, 2048], replicated
- shared_gate: bfloat16 [2048], replicated
- expert_w1: bfloat16 [64, 2048, 1408], P('ep')
- expert_w3: bfloat16 [64, 2048, 1408], P('ep')
- expert_w2: bfloat16 [64, 1408, 2048], P('ep')
Outputs:
- output: bfloat16 [4096, 2048], P(('dp', 'ep')), parts along dimension 0
There are 4 independent parts. A program takes and returns all parts, laid end to end along the dimension named above; an argument that names none is the same for every part.
All inputs are finite; a program needn't handle non-finite values.
Results may differ from a plain program's by a relative error of at most 0.00518169.
Values are sent between devices in bfloat16 or wider.
A program may use at most 1.25 GiB of HBM per device.

v0:
```python
import jax
import jax.numpy as jnp
from jax import lax
from jax.sharding import PartitionSpec as P


def solution(mesh):
    num_ep = mesh.shape['ep']
    row_spec = P(('dp', 'ep'), None)
    replicated = P()
    expert_spec = P('ep', None, None)

    def device_step(tokens, expert_ids, gate_vals, slots, shared_w1, shared_w3, shared_w2, shared_gate, expert_w1, expert_w3, expert_w2):
        tok_count, hidden = tokens.shape
        top_k = expert_ids.shape[1]
        local_experts = expert_w1.shape[0]
        num_experts = local_experts * num_ep
        capacity = 8 * ((2 * tok_count * top_k + 8 * num_experts - 1) // (8 * num_experts))
        buf_rows = num_experts * capacity
        kept_mask = slots >= 0
        slot_dest = jnp.where(kept_mask, expert_ids * capacity + slots, buf_rows)
        copy_tok = jnp.arange(tok_count * top_k, dtype=jnp.int32) // top_k
        row_owner = jnp.full((buf_rows + 1,), tok_count, jnp.int32).at[slot_dest.reshape(-1)].set(copy_tok)
        send_buf = jnp.take(tokens, row_owner[:buf_rows], axis=0, mode='fill', fill_value=0)
        recv_buf = lax.all_to_all(send_buf.reshape(num_ep, local_experts * capacity, hidden), 'ep', 0, 0, tiled=True)
        expert_in = recv_buf.reshape(num_ep, local_experts, capacity, hidden)
        act_a = jnp.einsum('secd,edf->secf', expert_in, expert_w1, preferred_element_type=jnp.float32)
        act_b = jnp.einsum('secd,edf->secf', expert_in, expert_w3, preferred_element_type=jnp.float32)
        hidden_act = (jax.nn.silu(act_a) * act_b).astype(jnp.bfloat16)
        expert_out = jnp.einsum('secf,efd->secd', hidden_act, expert_w2, preferred_element_type=jnp.float32).astype(jnp.bfloat16)
        back_buf = lax.all_to_all(expert_out.reshape(num_ep, local_experts * capacity, hidden), 'ep', 0, 0, tiled=True)
        picked = jnp.take(back_buf.reshape(buf_rows, hidden), slot_dest, axis=0, mode='fill', fill_value=0)
        weights = jnp.where(kept_mask, gate_vals, 0.0)[:, :, None]
        routed = jnp.sum(weights * picked, axis=1)
        gate_logit = jnp.dot(tokens, shared_gate, preferred_element_type=jnp.float32)
        shared_a = jnp.dot(tokens, shared_w1, preferred_element_type=jnp.float32)
        shared_b = jnp.dot(tokens, shared_w3, preferred_element_type=jnp.float32)
        shared_h = (jax.nn.silu(shared_a) * shared_b).astype(jnp.bfloat16)
        shared_out = jnp.dot(shared_h, shared_w2, preferred_element_type=jnp.float32)
        total = tokens.astype(jnp.float32) + jax.nn.sigmoid(gate_logit)[:, None] * shared_out + routed
        return total.astype(jnp.bfloat16)

    return jax.shard_map(device_step, mesh=mesh, in_specs=(row_spec, row_spec, row_spec, row_spec, replicated, replicated, replicated, replicated, expert_spec, expert_spec, expert_spec), out_specs=row_spec, check_vma=False)
```

profile of v0, /device:TPU:0, one launch (start us, length us, event | category | flops | bytes accessed | tf_op | source)
XLA Modules:
  0.0 518.6 jit_solution(10581298009872010759)
XLA Ops:
  0.0 1.3 compare_and_fusion.1
  1.3 0.0 copy-start.1
  1.3 0.1 copy.16
  1.4 0.1 reshape.60
  1.6 6.2 %scatter_custom_fusion = s32[3073]{0:T(1024)S(1)} fusion(s32[1536]{0:T(1024)S(1)} %fusion.26, s32[1536]{0:T(1024)S(1)} %add_select_fusion, s32[]{:T(128)} %constant.39.clone.1), kind=kCustom, calls=%fused_computation.40 | custom fusion | bytes 12296 | tf_op jit(solution)/shard_map/scatter | solution.py:23
  7.9 25.2 %gather_fusion = bf16[3072,2048]{1,0:T(8,128)(2,1)} fusion(bf16[256,2048]{1,0:T(8,128)(2,1)} %param.11, s32[3072]{0:T(1024)S(1)} %get-tuple-element.8), kind=kCustom, calls=%fused_computation | custom fusion | bytes 25178112 | tf_op jit(solution)/shard_map/jit(_take)/gather | solution.py:24
  33.0 0.0 copy-done.1
  33.0 6.3 %broadcast_select_fusion = bf16[4,768,2048]{2,1,0:T(8,128)(2,1)S(1)} fusion(bf16[4,768,2048]{2,1,0:T(8,128)(2,1)} %bitcast.52, pred[4,768]{1,0:T(4,128)(4,1)S(1)} %compare_and_fusion), kind=kLoop, calls=%fused_computation.18 | loop fusion | flops 6291456 | bytes 25168896 | tf_op jit(solution)/shard_map/jit(_take)/select_n | solution.py:24
  39.4 143.0 %all_to_all.10 = bf16[4,768,2048]{2,1,0:T(8,128)(2,1)} all-to-all(bf16[4,768,2048]{2,1,0:T(8,128)(2,1)S(1)} %broadcast_select_fusion), channel_id=1, replica_groups=mesh['dp'=4,'ep'=4] {'ep'}, dimensions={0} | all-to-all | bytes 25165824 | tf_op jit(solution)/shard_map/all_to_all | solution.py:25
  182.4 40.5 %fusion.2 = f32[16,4,48,1408]{3,2,1,0:T(8,128)} fusion(bf16[16,2048,1408]{2,1,0:T(8,128)(2,1)} %param.20, bf16[4,16,48,2048]{3,2,1,0:T(8,128)(2,1)} %bitcast.53), kind=kOutput, calls=%fused_computation.5 | convolution fusion | flops 17716740096 | bytes 122159104 | tf_op jit(solution)/shard_map/secd,edf->secf/dot_general | solution.py:28
  222.8 46.1 %fusion.6 = bf16[4,16,48,1408]{3,2,0,1:T(8,128)(2,1)} fusion(f32[16,4,48,1408]{3,2,1,0:T(8,128)} %fusion.2, bf16[16,2048,1408]{2,1,0:T(8,128)(2,1)} %param.19, bf16[4,16,48,2048]{3,2,1,0:T(8,128)(2,1)} %bitcast.54), kind=kOutput, calls=%fused_computation.10 | convolution fusion | flops 17742692352 | bytes 130809856 | tf_op jit(solution)/shard_map/secd,edf->secf/dot_general | solution.py:27
  268.9 38.6 %convert_bitcast_fusion = bf16[4,16,48,2048]{3,2,0,1:T(8,128)(2,1)} fusion(bf16[4,16,48,1408]{3,2,0,1:T(8,128)(2,1)} %fusion.6, bf16[16,1408,2048]{2,1,0:T(8,128)(2,1)} %param.21), kind=kOutput, calls=%fused_computation.17 | convolution fusion | flops 17723031552 | bytes 113508352 | tf_op jit(solution)/shard_map/secf,efd->secd/dot_general | solution.py:30
  307.6 10.7 %copy.18 = bf16[4,16,48,2048]{3,2,1,0:T(8,128)(2,1)} copy(bf16[4,16,48,2048]{3,2,0,1:T(8,128)(2,1)} %convert_bitcast_fusion) | data formatting | bytes 25165824 | tf_op jit(solution)/shard_map/convert_element_type | solution.py:30
  318.3 0.0 copy-start.2
  318.3 0.0 copy-start.5
  318.3 0.0 copy-start.3
  318.3 0.0 copy-start.4
  318.3 0.0 copy-start.6
  318.3 0.0 copy-start
  318.3 6.6 %all-to-all-start.1 = ((bf16[4,768,2048]{2,1,0:T(8,128)(2,1)}), bf16[4,768,2048]{2,1,0:T(8,128)(2,1)}, u32[]{:S(2)}, u32[]{:S(2)}) async-start(bf16[4,768,2048]{2,1,0:T(8,128)(2,1)} %bitcast.51), calls=%async_computation.1 | async-start | bytes 25165824 | tf_op jit(solution)/shard_map/all_to_all | solution.py:31
  325.0 0.0 copy-done.2
  325.0 0.1 copy.19
  325.1 0.1 reshape.74
  325.3 0.0 copy-done.5
  325.3 0.2 copy.15
  325.5 0.0 copy-done.3
  325.5 0.0 copy-done.4
  325.5 0.1 copy.14
  325.7 0.0 copy-done.6
  325.7 0.0 copy-done
  325.7 0.4 fusion.29
  326.1 9.1 %fusion.30 = f32[256,2816]{1,0:T(8,128)} fusion(bf16[256,2048]{1,0:T(8,128)(2,1)S(1)} %copy-done, bf16[2048,2816]{1,0:T(8,128)(2,1)} %param.15), kind=kOutput, calls=%fused_computation.52 | convolution fusion | flops 2952790016 | bytes 15466496 | tf_op jit(solution)/shard_map/dot_general | solution.py:36
  335.2 127.4 %all-to-all-done.1 = bf16[4,768,2048]{2,1,0:T(8,128)(2,1)} async-done(((bf16[4,768,2048]{2,1,0:T(8,128)(2,1)}), bf16[4,768,2048]{2,1,0:T(8,128)(2,1)}, u32[]{:S(2)}, u32[]{:S(2)}) %all-to-all-start.1) | async-done | bytes 12582944 | tf_op jit(solution)/shard_map/all_to_all | solution.py:31
  462.6 18.9 %gather_fusion.1 = bf16[1536,2048]{1,0:T(8,128)(2,1)} fusion(bf16[3072,2048]{1,0:T(8,128)(2,1)} %bitcast.13, s32[2048]{0:T(1024)S(1)} %pad_clamp_fusion), kind=kCustom, calls=%fused_computation.1 | custom fusion | bytes 12589056 | tf_op jit(solution)/shard_map/jit(_take)/gather | solution.py:32
  481.5 11.0 %reshape.73 = bf16[256,6,2048]{2,1,0:T(8,128)(2,1)} reshape(bf16[1536,2048]{1,0:T(8,128)(2,1)} %gather_fusion.1) | data formatting | bytes 12582912 | tf_op jit(solution)/shard_map/jit(_take)/gather | solution.py:32
  492.5 10.5 %multiply_reduce_fusion = f32[256,2048]{1,0:T(8,128)S(1)} fusion(bf16[256,6,2048]{2,1,0:T(8,128)(2,1)} %reshape.73, f32[256,6]{1,0:T(8,128)S(1)} %copy.14, pred[256,6]{1,0:T(8,128)(4,1)S(1)} %copy.15), kind=kLoop, calls=%fused_computation.16 | loop fusion | flops 12058624 | bytes 8396288 | tf_op jit(solution)/shard_map/reduce_sum | solution.py:34
  503.0 15.6 %fusion.19 = bf16[256,2048]{1,0:T(8,128)(2,1)} fusion(f32[256,2048]{1,0:T(8,128)S(1)} %multiply_reduce_fusion, bf16[2816,2048]{1,0:T(8,128)(2,1)} %param.17, bf16[256,2048]{1,0:T(8,128)(2,1)S(1)} %copy-done, f32[256]{0:T(256)S(1)} %add_divide_fusion, bf16[2048,2816]{1,0:T(8,128)(2,1)} %param.16, f32[256,2816]{1,0:T(8,128)} %fusion.30), kind=kOutput, calls=%fused_computation.26 | convolution fusion | flops 5912526848 | bytes 30147584 | tf_op jit(solution)/shard_map/dot_general | solution.py:39
  (10 shorter events, 0.1 us)
Async XLA Ops:
  1.3 31.8 %copy-start.1 = (s32[256,6]{0,1:T(8,128)}, s32[256,6]{0,1:T(8,128)S(1)}, u32[]{:S(2)}) copy-start(s32[256,6]{0,1:T(8,128)S(1)} %get-tuple-element.6) | copy-start | bytes 18436
  318.3 6.7 %copy-start.2 = (s32[256,6]{0,1:T(8,128)S(1)}, s32[256,6]{0,1:T(8,128)}, u32[]{:S(2)}) copy-start(s32[256,6]{0,1:T(8,128)} %copy-done.1) | copy-start | bytes 18436
  318.3 7.0 %copy-start.5 = (pred[256,6]{0,1:T(8,128)(4,1)S(1)}, pred[256,6]{0,1:T(8,128)(4,1)}, u32[]{:S(2)}) copy-start(pred[256,6]{0,1:T(8,128)(4,1)} %get-tuple-element.5) | copy-start | bytes 4612
  318.3 7.2 %copy-start.3 = (s32[256,6]{0,1:T(8,128)S(1)}, s32[256,6]{0,1:T(8,128)}, u32[]{:S(2)}) copy-start(s32[256,6]{0,1:T(8,128)} %param.14) | copy-start | bytes 18436
  318.3 7.2 %copy-start.4 = (f32[256,6]{0,1:T(8,128)S(1)}, f32[256,6]{0,1:T(8,128)}, u32[]{:S(2)}) copy-start(f32[256,6]{0,1:T(8,128)} %param.13) | copy-start | bytes 18436
  318.3 7.3 %copy-start.6 = (bf16[2048]{0:T(1024)(128)(2,1)S(1)}, bf16[2048]{0:T(1024)(128)(2,1)}, u32[]{:S(2)}) copy-start(bf16[2048]{0:T(1024)(128)(2,1)} %param.18) | copy-start | bytes 12292
  318.3 7.4 %copy-start = (bf16[256,2048]{1,0:T(8,128)(2,1)S(1)}, bf16[256,2048]{1,0:T(8,128)(2,1)}, u32[]{:S(2)}) copy-start(bf16[256,2048]{1,0:T(8,128)(2,1)} %param.11) | copy-start | bytes 3145732
  318.3 144.2 %all-to-all-start.1 = ((bf16[4,768,2048]{2,1,0:T(8,128)(2,1)}), bf16[4,768,2048]{2,1,0:T(8,128)(2,1)}, u32[]{:S(2)}, u32[]{:S(2)}) async-start(bf16[4,768,2048]{2,1,0:T(8,128)(2,1)} %bitcast.51), calls=%async_computation.1 | async-start | bytes 25165824 | tf_op jit(solution)/shard_map/all_to_all | solution.py:31
where the time goes:
time: 519 us
  matrix products  150 us (29%)
  blocking collectives  143 us (28%)
  waiting for transfers between devices  127 us (24%)
  local copies, waits for them, and re-layouts  72.9 us (14%)
  other arithmetic  18.2 us (4%)
  starting transfers between devices  6.64 us (1%)
    all_to_all x1, blocking collectives, device_step(): lax.all_to_all(send_buf.reshape(num_ep, local_experts * capacity, hidden)...  143 us
    all_to_all x1, waiting for transfers between devices, device_step(): lax.all_to_all(expert_out.reshape(num_ep, local_experts * capacity, hidde...  127 us
    dot_general x1, matrix products, device_step(): jnp.einsum('secd,edf->secf', expert_in, expert_w1, preferred_element_type...  46.1 us
    dot_general x1, matrix products, device_step(): jnp.einsum('secd,edf->secf', expert_in, expert_w3, preferred_element_type...  40.5 us
    dot_general x1, matrix products, device_step(): jnp.einsum('secf,efd->secd', hidden_act, expert_w2, preferred_element_typ...  38.6 us
    gather x2, local copies, waits for them, and re-layouts, device_step(): jnp.take(back_buf.reshape(buf_rows, hidden), slot_dest, axis=0, mode='fil...  29.9 us
    gather x1, local copies, waits for them, and re-layouts, device_step(): jnp.take(tokens, row_owner[:buf_rows], axis=0, mode='fill', fill_value=0)  25.2 us
    dot_general x1, matrix products, device_step(): jnp.dot(shared_h, shared_w2, preferred_element_type=jnp.float32)  15.6 us
  transfers between devices with their start and end apart: 1, of which 1 were waited for; matrix products, arithmetic and copies ran while one was open for 2% of the time, Pallas kernels for 0%

commit v1 on v0

v1 whole, which is shorter than its diff:
```python
import functools

import jax
import jax.numpy as jnp
from jax import lax
from jax.experimental import pallas as pl
from jax.experimental.pallas import tpu as pltpu
from jax.sharding import PartitionSpec as P

MESH = pl.DeviceIdType.MESH
F32 = jnp.float32
BF16 = jnp.bfloat16
CHUNK = 256
RING = 5
PIECES = 4
GROUP = 4
LAG = 2
BF16_MAX = 3.3895313892515355e38


def moe_kernel(cfg, tok, route, sgate, sw1, sw3, sw2, ew1, ew3, ew2, y,
               toks, rts, wbuf, xg, h, hs, gs, rbuf, sig, acc, send3, send1, recv3, recv1, recvu,
               load_sem, wsem, tsem, tok_send, tok_recv, rt_send, rt_recv,
               s3_send, s1_send, su_send, r3_sem, r1_sem, ru_sem):
    n_tok, hidden, n_exp, ff, cap, top_k = cfg
    rows = 4 * cap
    n_chunks = hidden // CHUNK
    per_slot = ff // CHUNK
    n_sub = RING * per_slot
    n_items = 2 * (n_exp + 2)
    per_chunk = n_exp + 2
    n_tiles = n_chunks * per_chunk
    piece = n_tok // PIECES
    slots_all = n_exp * cap

    dp = lax.axis_index('dp')
    me = lax.axis_index('ep')
    partner = (dp, me + 1 - 2 * lax.rem(me, 2))
    across = (dp, lax.rem(me + 2, 4))
    diagonal = (dp, 3 - me)

    def item_copy(item, slot):
        def desc(src):
            return pltpu.make_async_copy(src, wbuf.at[slot], wsem.at[slot])
        return desc

    def shared_item(item):
        src = (sw1, sw3)[item % 2].at[:, pl.ds((item // 2) * ff, ff)]
        return pltpu.make_async_copy(src, wbuf.at[item % RING], wsem.at[item % RING])

    def expert_item(exp, which):
        slot = lax.rem(2 * exp + 4 + which, RING)
        return pltpu.make_async_copy((ew1, ew3)[which].at[exp], wbuf.at[slot], wsem.at[slot])

    def tile_dst(tile):
        sub = lax.rem(tile, n_sub)
        slot = lax.rem(1 + sub // per_slot, RING)
        lane = pl.multiple_of(lax.rem(sub, per_slot) * CHUNK, CHUNK)
        return slot, lane, sub

    def tile_view(tile):
        slot, lane, sub = tile_dst(tile)
        return wbuf.at[slot, pl.ds(0, ff), pl.ds(lane, CHUNK)], tsem.at[sub]

    def start_tile(tile):
        chunk, idx = tile // per_chunk, lax.rem(tile, per_chunk)
        col = pl.ds(pl.multiple_of(chunk * CHUNK, CHUNK), CHUNK)
        dst, sem = tile_view(tile)

        @pl.when(idx < n_exp)
        def _():
            pltpu.make_async_copy(ew2.at[idx, :, col], dst, sem).start()

        @pl.when(idx >= n_exp)
        def _():
            row = pl.multiple_of((idx - n_exp) * ff, 128)
            pltpu.make_async_copy(sw2.at[pl.ds(row, ff), col], dst, sem).start()

    def wait_tile(tile):
        dst, sem = tile_view(tile)
        pltpu.make_async_copy(ew2.at[0, :, pl.ds(0, CHUNK)], dst, sem).wait()

    def load_tile(tile):
        slot, lane, _ = tile_dst(tile)
        return wbuf[slot, pl.ds(0, ff), pl.ds(lane, CHUNK)]

    own_load = pltpu.make_async_copy(tok, toks.at[0], load_sem)
    own_load.start()
    for item in range(4):
        shared_item(item).start()
    expert_item(0, 0).start()

    barrier = pltpu.get_barrier_semaphore()
    for peer in (partner, across, diagonal):
        pl.semaphore_signal(barrier, inc=1, device_id=peer, device_id_type=MESH)
    pl.semaphore_wait(barrier, 3)
    own_load.wait()

    def remote(src, dst, send, recv, peer):
        return pltpu.make_async_remote_copy(src_ref=src, dst_ref=dst, send_sem=send, recv_sem=recv,
                                            device_id=peer, device_id_type=MESH)

    def piece_of(ref, i):
        return ref.at[pl.ds(i * piece, piece)]

    rt_copies = [remote(route, rts.at[d], rt_send.at[d], rt_recv.at[d], peer)
                 for d, peer in ((1, partner), (2, across), (3, diagonal))]
    for copy in rt_copies:
        copy.start()
    tok_across = [remote(piece_of(toks.at[0], i), piece_of(toks.at[2], i), tok_send.at[i], tok_recv.at[i], across)
                  for i in range(PIECES)]
    for copy in tok_across:
        copy.start()
    tok_partner = remote(toks.at[0], toks.at[1], tok_send.at[2 * PIECES], tok_recv.at[2 * PIECES], partner)
    tok_partner.start()
    tok_relay = [remote(piece_of(toks.at[2], i), piece_of(toks.at[3], i), tok_send.at[PIECES + i],
                        tok_recv.at[PIECES + i], partner) for i in range(PIECES)]

    def swiglu_cols(x, slot1, slot3, store):
        def block(i, carry):
            col = pl.multiple_of(i * CHUNK, CHUNK)
            a = jnp.dot(x(), wbuf[slot1, :, pl.ds(col, CHUNK)], preferred_element_type=F32)
            b = jnp.dot(x(), wbuf[slot3, :, pl.ds(col, CHUNK)], preferred_element_type=F32)
            store(col, CHUNK, (jax.nn.silu(a) * b).astype(BF16))
            return carry
        lax.fori_loop(0, per_slot, block, 0)
        done = per_slot * CHUNK
        rest = ff - done
        w = jnp.concatenate([wbuf[slot1, :, pl.ds(done, rest)], wbuf[slot3, :, pl.ds(done, rest)]], axis=1)
        ab = jnp.dot(x(), w, preferred_element_type=F32)
        store(done, rest, (jax.nn.silu(ab[:, :rest]) * ab[:, rest:]).astype(BF16))

    for half in range(2):
        shared_item(2 * half).wait()
        shared_item(2 * half + 1).wait()

        def store_shared(col, width, value):
            hs[half, :, pl.ds(col, width)] = value

        swiglu_cols(lambda: toks[0], (2 * half) % RING, (2 * half + 1) % RING, store_shared)
        expert_item(half, 1).start()
        expert_item(half + 1, 0).start()

    logit = jnp.sum(toks[0].astype(F32) * sgate[...].astype(F32), axis=1, keepdims=True)
    sig[...] = jnp.broadcast_to(jax.nn.sigmoid(logit), sig.shape)

    for copy in rt_copies:
        copy.wait_recv()
    tok_partner.wait_recv()
    base = (me * slots_all).astype(F32)

    def route_rows(d):
        return route if d == 0 else rts.at[d]

    for d in range(4):
        def weight_block(i, carry):
            row = (lax.broadcasted_iota(jnp.int32, (128, n_tok), 0) + i * 128).astype(F32) + base
            g = jnp.zeros((128, n_tok), F32)
            for k in range(top_k):
                g += jnp.where(row == route_rows(d)[k:k + 1, :], route_rows(d)[8 + k:9 + k, :], 0.0)
            g = g.T
            g1 = jnp.minimum(g, BF16_MAX).astype(BF16)
            left = g - g1.astype(F32)
            g2 = left.astype(BF16)
            g3 = (left - g2.astype(F32)).astype(BF16)
            for part, value in enumerate((g1, g2, g3)):
                gs[d, :, pl.ds(pl.multiple_of(part * slots_all + i * 128, 128), 128)] = value
            return carry
        lax.fori_loop(0, slots_all // 128, weight_block, 0)

    for arrived, relay in zip(tok_across, tok_relay):
        arrived.wait_recv()
        relay.start()
    for relay in tok_relay:
        relay.wait_recv()

    def group_step(g, carry):
        for d in range(4):
            row = (lax.broadcasted_iota(jnp.int32, (GROUP * cap, n_tok), 0) + g * (GROUP * cap)).astype(F32) + base
            pick = jnp.zeros((GROUP * cap, n_tok), F32)
            for k in range(top_k):
                pick += jnp.where(row == route_rows(d)[k:k + 1, :], 1.0, 0.0)
            pick = pick.astype(BF16)

            def gather_cols(i, carry):
                col = pl.ds(pl.multiple_of(i * 512, 512), 512)
                got = jnp.dot(pick, toks[d, :, col], preferred_element_type=F32).astype(BF16)
                for e in range(GROUP):
                    xg[e, pl.ds(d * cap, cap), col] = got[e * cap:(e + 1) * cap]
                return carry
            lax.fori_loop(0, hidden // 512, gather_cols, 0)

        def expert_step(i, carry):
            exp = g * GROUP + i
            expert_item(exp, 0).wait()
            expert_item(exp, 1).wait()

            def store_h(col, width, value):
                h[exp, :, pl.ds(col, width)] = value

            slot1, slot3 = lax.rem(2 * exp + 4, RING), lax.rem(2 * exp + 5, RING)
            swiglu_cols(lambda: xg[i], slot1, slot3, store_h)

            @pl.when(exp + 2 < n_exp)
            def _():
                expert_item(exp + 2, 1).start()

            @pl.when(exp + 3 < n_exp)
            def _():
                expert_item(exp + 3, 0).start()

            @pl.when(exp == n_exp - 3)
            def _():
                for t in range(per_slot):
                    start_tile(jnp.int32(t))

            @pl.when(exp == n_exp - 2)
            def _():
                for t in range(per_slot, 3 * per_slot):
                    start_tile(jnp.int32(t))

            @pl.when(exp == n_exp - 1)
            def _():
                for t in range(3 * per_slot, 5 * per_slot):
                    start_tile(jnp.int32(t))
            return carry
        lax.fori_loop(0, GROUP, expert_step, 0)
        return carry
    lax.fori_loop(0, n_exp // GROUP, group_step, 0)

    def next_tile(tile):
        @pl.when(tile + n_sub < n_tiles)
        def _():
            start_tile(tile + n_sub)

    def combine(d):
        r = rbuf[d]
        return jnp.dot(gs[d], jnp.concatenate([r, r, r], axis=0), preferred_element_type=F32)

    def to_partner3(j):
        return remote(send3.at[lax.rem(j, 2)], recv3.at[j], s3_send.at[lax.rem(j, 2)], r3_sem.at[j], partner)

    def to_partner1(j):
        return remote(send1.at[lax.rem(j, 2)], recv1.at[j], s1_send.at[lax.rem(j, 2)], r1_sem.at[j], partner)

    def to_across(j):
        return remote(recv3.at[j], recvu.at[j], su_send.at[j], ru_sem.at[j], across)

    def finish(j):
        to_partner1(j).wait_recv()
        to_across(j).wait_recv()
        col = pl.ds(pl.multiple_of(j * CHUNK, CHUNK), CHUNK)
        y[:, col] = (acc[j] + recv1[j] + recvu[j]).astype(y.dtype)

    def chunk_step(j, carry):
        first = j * per_chunk

        def pair_step(i, carry):
            tile = first + 2 * i
            wait_tile(tile)
            wait_tile(tile + 1)
            for u in range(2):
                exp = 2 * i + u
                r = jnp.dot(h[exp], load_tile(tile + u), preferred_element_type=F32).astype(BF16)
                for d in range(4):
                    rbuf[d, pl.ds(pl.multiple_of(exp * cap, 16), cap), :] = r[d * cap:(d + 1) * cap]
            next_tile(tile)
            next_tile(tile + 1)
            return carry
        lax.fori_loop(0, n_exp // 2, pair_step, 0)

        @pl.when(j >= 2)
        def _():
            to_partner3(j - 2).wait_send()
            to_partner1(j - 2).wait_send()
        send3[lax.rem(j, 2)] = combine(3)
        to_partner3(j).start()
        send1[lax.rem(j, 2)] = combine(1)
        to_partner1(j).start()
        part2 = combine(2)
        to_partner3(j).wait_recv()
        recv3[j] = recv3[j] + part2
        to_across(j).start()

        tile = first + n_exp
        wait_tile(tile)
        wait_tile(tile + 1)
        s = (jnp.dot(hs[0], load_tile(tile), preferred_element_type=F32)
             + jnp.dot(hs[1], load_tile(tile + 1), preferred_element_type=F32))
        next_tile(tile)
        next_tile(tile + 1)
        col = pl.ds(pl.multiple_of(j * CHUNK, CHUNK), CHUNK)
        acc[j] = toks[0, :, col].astype(F32) + sig[:, 0:1] * s + combine(0)

        @pl.when(j >= LAG)
        def _():
            finish(j - LAG)
        return carry
    lax.fori_loop(0, n_chunks, chunk_step, 0)

    def last_step(j, carry):
        finish(j)
        return carry
    lax.fori_loop(n_chunks - LAG, n_chunks, last_step, 0)

    for copy in rt_copies + tok_across + tok_relay + [tok_partner]:
        copy.wait_send()
    for j in range(n_chunks - 2, n_chunks):
        to_partner3(j).wait_send()
        to_partner1(j).wait_send()

    def drain(j, carry):
        to_across(j).wait_send()
        return carry
    lax.fori_loop(0, n_chunks, drain, 0)


def solution(mesh):
    num_ep = mesh.shape['ep']
    row_spec = P(('dp', 'ep'), None)
    expert_spec = P('ep', None, None)

    def device_step(tokens, expert_ids, gate_vals, slots, shared_w1, shared_w3, shared_w2, shared_gate, expert_w1, expert_w3, expert_w2):
        n_tok, hidden = tokens.shape
        top_k = expert_ids.shape[1]
        n_exp, _, ff = expert_w1.shape
        num_experts = n_exp * num_ep
        cap = 8 * ((2 * n_tok * top_k + 8 * num_experts - 1) // (8 * num_experts))
        rows = num_ep * cap
        n_chunks = hidden // CHUNK
        per_slot = ff // CHUNK

        dest = jnp.where(slots >= 0, expert_ids * cap + slots, -1).astype(F32)
        pad = ((0, 8 - top_k), (0, 0))
        route = jnp.concatenate([jnp.pad(dest.T, pad, constant_values=-1.0), jnp.pad(gate_vals.T, pad)], axis=0)

        anywhere = pl.BlockSpec(memory_space=pl.ANY)
        vmem = pl.BlockSpec(memory_space=pltpu.VMEM)
        dma = pltpu.SemaphoreType.DMA
        block = (n_tok, CHUNK)
        return pl.pallas_call(
            functools.partial(moe_kernel, (n_tok, hidden, n_exp, ff, cap, top_k)),
            out_shape=jax.ShapeDtypeStruct((n_tok, hidden), tokens.dtype),
            in_specs=[anywhere, vmem, vmem] + [anywhere] * 6,
            out_specs=vmem,
            scratch_shapes=[
                pltpu.VMEM((4, n_tok, hidden), BF16),
                pltpu.VMEM((4, 16, n_tok), F32),
                pltpu.VMEM((RING, hidden, ff), BF16),
                pltpu.VMEM((GROUP, rows, hidden), BF16),
                pltpu.VMEM((n_exp, rows, ff), BF16),
                pltpu.VMEM((2, n_tok, ff), BF16),
                pltpu.VMEM((4, n_tok, 3 * n_exp * cap), BF16),
                pltpu.VMEM((4, n_exp * cap, CHUNK), BF16),
                pltpu.VMEM((n_tok, 128), F32),
                pltpu.VMEM((n_chunks,) + block, F32),
                pltpu.VMEM((2,) + block, F32),
                pltpu.VMEM((2,) + block, F32),
                pltpu.VMEM((n_chunks,) + block, F32),
                pltpu.VMEM((n_chunks,) + block, F32),
                pltpu.VMEM((n_chunks,) + block, F32),
                dma, dma((RING,)), dma((RING * per_slot,)),
                dma((2 * PIECES + 1,)), dma((2 * PIECES + 1,)), dma((4,)), dma((4,)),
                dma((2,)), dma((2,)), dma((n_chunks,)),
                dma((n_chunks,)), dma((n_chunks,)), dma((n_chunks,)),
            ],
            compiler_params=pltpu.CompilerParams(collective_id=0, has_side_effects=True, vmem_limit_bytes=67043328),
        )(tokens, route, shared_gate.reshape(1, hidden), shared_w1, shared_w3, shared_w2, expert_w1, expert_w3, expert_w2)

    return jax.shard_map(device_step, mesh=mesh, in_specs=(row_spec, row_spec, row_spec, row_spec, P(), P(), P(), P(), expert_spec, expert_spec, expert_spec), out_specs=row_spec, check_vma=False)
```

time: 519 us -> 183 us (0.35)
  Pallas kernels: 0 us -> 177 us
  matrix products: 150 us -> 0 us
  blocking collectives: 143 us -> 0 us
  waiting for transfers between devices: 127 us -> 0 us
  local copies, waits for them, and re-layouts: 72.9 us -> 3.59 us
  other arithmetic: 18.2 us -> 2.02 us
  starting transfers between devices: 6.64 us -> 0 us
    pallas_call x0 -> x1, Pallas kernels: none -> 177 us  [device_step(): pl.pallas_call(functools.partial(moe_kernel, (n_tok, hidden, n_exp, ff, c...]
    dot_general x6 -> x0, matrix products: 150 us -> none  [the longest x1 46.1 us: device_step(): jnp.einsum('secd,edf->secf', expert_in, expert_w1, preferred_element_type...]
    all_to_all x1 -> x0, blocking collectives: 143 us -> none  [device_step(): lax.all_to_all(send_buf.reshape(num_ep, local_experts * capacity, hidden)...]
    all_to_all x1 -> x0, waiting for transfers between devices: 127 us -> none  [device_step(): lax.all_to_all(expert_out.reshape(num_ep, local_experts * capacity, hidde...]
    gather x3 -> x0, local copies, waits for them, and re-layouts: 55.1 us -> none  [the longest x2 29.9 us: device_step(): jnp.take(back_buf.reshape(buf_rows, hidden), slot_dest, axis=0, mode='fil...]
    convert_element_type x1 -> x0, local copies, waits for them, and re-layouts: 10.7 us -> none  [device_step(): jnp.einsum('secf,efd->secd', hidden_act, expert_w2, preferred_element_typ...]
    reduce_sum x1 -> x0, other arithmetic: 10.5 us -> none  [device_step(): routed = jnp.sum(weights * picked, axis=1)]
    all_to_all x1 -> x0, starting transfers between devices: 6.64 us -> none  [device_step(): lax.all_to_all(expert_out.reshape(num_ep, local_experts * capacity, hidde...]
  transfers between devices with their start and end apart: 1 -> 0, of which waited for: 1 -> 0; matrix products, arithmetic and copies ran while one was open for 2% -> 0% of each run, Pallas kernels for 0% -> 0%
where the time goes in v1:
time: 183 us; the launch traced here: 182 us
  Pallas kernels  177 us (97%)
  local copies, waits for them, and re-layouts  3.59 us (2%)
  other arithmetic  2.02 us (1%)
    pallas_call x1, Pallas kernels, device_step(): pl.pallas_call(functools.partial(moe_kernel, (n_tok, hidden, n_exp, ff, c...  177 us

profile of v1, /device:TPU:0, one launch (start us, length us, event | category | flops | bytes accessed | tf_op | source)
XLA Modules:
  0.0 182.2 jit_solution(6847449900336290697)
XLA Ops:
  0.0 0.7 convert_bitcast_fusion
  0.7 1.3 select_maximum_fusion.route
  2.0 1.3 reshape.3.sgate
  3.3 176.5 %shard_map.109 = bf16[256,2048]{1,0:T(8,128)(2,1)} custom-call(bf16[256,2048]{1,0:T(8,128)(2,1)} %tok.1, f32[16,256]{1,0:T(8,128)} %select_maximum_fusion.route, bf16[1,2048]{1,0:T(2,128)(2,1)} %reshape.3.sgate, bf16[2048,2816]{1,0:T(8,128)(2,1)} %sw1.1, bf16[2048,2816]{1,0:T(8,128)(2,1)} %sw3.1, bf16[2816,2048]{1,0:T(8,128)(2,1)} %sw2.1, ...), custom_call_target="tpu_custom_call" | custom-call | tf_op jit(solution)/shard_map/pallas_call | solution.py:341
  179.9 2.3 %copy.13 = bf16[256,2048]{1,0:T(8,128)(2,1)} copy(bf16[256,2048]{1,0:T(8,128)(2,1)} %shard_map.109) | data formatting | bytes 2097152

commit v2 on v1

--- a/solution.py
+++ b/solution.py
@@ -15,6 +15,7 @@
 PIECES = 4
 GROUP = 4
 LAG = 2
+BATCH = 8
 BF16_MAX = 3.3895313892515355e38
 
 
@@ -23,7 +24,6 @@
                load_sem, wsem, tsem, tok_send, tok_recv, rt_send, rt_recv,
                s3_send, s1_send, su_send, r3_sem, r1_sem, ru_sem):
     n_tok, hidden, n_exp, ff, cap, top_k = cfg
-    rows = 4 * cap
     n_chunks = hidden // CHUNK
     per_slot = ff // CHUNK
     n_sub = RING * per_slot
@@ -39,11 +39,6 @@
     across = (dp, lax.rem(me + 2, 4))
     diagonal = (dp, 3 - me)
 
-    def item_copy(item, slot):
-        def desc(src):
-            return pltpu.make_async_copy(src, wbuf.at[slot], wsem.at[slot])
-        return desc
-
     def shared_item(item):
         src = (sw1, sw3)[item % 2].at[:, pl.ds((item // 2) * ff, ff)]
         return pltpu.make_async_copy(src, wbuf.at[item % RING], wsem.at[item % RING])
@@ -86,15 +81,16 @@
 
     own_load = pltpu.make_async_copy(tok, toks.at[0], load_sem)
     own_load.start()
+    barrier = pltpu.get_barrier_semaphore()
+    for peer in (partner, across, diagonal):
+        pl.semaphore_signal(barrier, inc=1, device_id=peer, device_id_type=MESH)
+    with jax.named_scope('own_load'):
+        own_load.wait()
     for item in range(4):
         shared_item(item).start()
     expert_item(0, 0).start()
-
-    barrier = pltpu.get_barrier_semaphore()
-    for peer in (partner, across, diagonal):
-        pl.semaphore_signal(barrier, inc=1, device_id=peer, device_id_type=MESH)
-    pl.semaphore_wait(barrier, 3)
-    own_load.wait()
+    with jax.named_scope('barrier'):
+        pl.semaphore_wait(barrier, 3)
 
     def remote(src, dst, send, recv, peer):
         return pltpu.make_async_remote_copy(src_ref=src, dst_ref=dst, send_sem=send, recv_sem=recv,
@@ -117,13 +113,11 @@
                         tok_recv.at[PIECES + i], partner) for i in range(PIECES)]
 
     def swiglu_cols(x, slot1, slot3, store):
-        def block(i, carry):
-            col = pl.multiple_of(i * CHUNK, CHUNK)
+        for i in range(per_slot):
+            col = i * CHUNK
             a = jnp.dot(x(), wbuf[slot1, :, pl.ds(col, CHUNK)], preferred_element_type=F32)
             b = jnp.dot(x(), wbuf[slot3, :, pl.ds(col, CHUNK)], preferred_element_type=F32)
             store(col, CHUNK, (jax.nn.silu(a) * b).astype(BF16))
-            return carry
-        lax.fori_loop(0, per_slot, block, 0)
         done = per_slot * CHUNK
         rest = ff - done
         w = jnp.concatenate([wbuf[slot1, :, pl.ds(done, rest)], wbuf[slot3, :, pl.ds(done, rest)]], axis=1)
@@ -182,13 +176,11 @@
                 pick += jnp.where(row == route_rows(d)[k:k + 1, :], 1.0, 0.0)
             pick = pick.astype(BF16)
 
-            def gather_cols(i, carry):
-                col = pl.ds(pl.multiple_of(i * 512, 512), 512)
+            for i in range(hidden // 512):
+                col = pl.ds(i * 512, 512)
                 got = jnp.dot(pick, toks[d, :, col], preferred_element_type=F32).astype(BF16)
                 for e in range(GROUP):
                     xg[e, pl.ds(d * cap, cap), col] = got[e * cap:(e + 1) * cap]
-                return carry
-            lax.fori_loop(0, hidden // 512, gather_cols, 0)
 
         def expert_step(i, carry):
             exp = g * GROUP + i
@@ -255,42 +247,41 @@
     def chunk_step(j, carry):
         first = j * per_chunk
 
-        def pair_step(i, carry):
-            tile = first + 2 * i
-            wait_tile(tile)
-            wait_tile(tile + 1)
-            for u in range(2):
-                exp = 2 * i + u
+        def batch_step(i, carry):
+            tile = first + BATCH * i
+            for u in range(BATCH):
+                wait_tile(tile + u)
+            for u in range(BATCH):
+                exp = BATCH * i + u
                 r = jnp.dot(h[exp], load_tile(tile + u), preferred_element_type=F32).astype(BF16)
                 for d in range(4):
                     rbuf[d, pl.ds(pl.multiple_of(exp * cap, 16), cap), :] = r[d * cap:(d + 1) * cap]
-            next_tile(tile)
-            next_tile(tile + 1)
+            for u in range(BATCH):
+                next_tile(tile + u)
             return carry
-        lax.fori_loop(0, n_exp // 2, pair_step, 0)
+        lax.fori_loop(0, n_exp // BATCH, batch_step, 0)
 
         @pl.when(j >= 2)
         def _():
             to_partner3(j - 2).wait_send()
             to_partner1(j - 2).wait_send()
+        tile = first + n_exp
+        wait_tile(tile)
+        wait_tile(tile + 1)
         send3[lax.rem(j, 2)] = combine(3)
+        send1[lax.rem(j, 2)] = combine(1)
         to_partner3(j).start()
-        send1[lax.rem(j, 2)] = combine(1)
         to_partner1(j).start()
         part2 = combine(2)
+        s = (jnp.dot(hs[0], load_tile(tile), preferred_element_type=F32)
+             + jnp.dot(hs[1], load_tile(tile + 1), preferred_element_type=F32))
+        col = pl.ds(pl.multiple_of(j * CHUNK, CHUNK), CHUNK)
+        acc[j] = toks[0, :, col].astype(F32) + sig[:, 0:1] * s + combine(0)
         to_partner3(j).wait_recv()
         recv3[j] = recv3[j] + part2
         to_across(j).start()
-
-        tile = first + n_exp
-        wait_tile(tile)
-        wait_tile(tile + 1)
-        s = (jnp.dot(hs[0], load_tile(tile), preferred_element_type=F32)
-             + jnp.dot(hs[1], load_tile(tile + 1), preferred_element_type=F32))
         next_tile(tile)
         next_tile(tile + 1)
-        col = pl.ds(pl.multiple_of(j * CHUNK, CHUNK), CHUNK)
-        acc[j] = toks[0, :, col].astype(F32) + sig[:, 0:1] * s + combine(0)
 
         @pl.when(j >= LAG)
         def _():

time: 183 us -> 146 us (0.80)
  Pallas kernels: 177 us -> 140 us
    pallas_call x1, Pallas kernels: 177 us -> 140 us  [device_step(): pl.pallas_call(functools.partial(moe_kernel, (n_tok, hidden, n_exp, ff, c...]
where the time goes in v2:
time: 146 us
  Pallas kernels  140 us (96%)
  local copies, waits for them, and re-layouts  3.59 us (2%)
  other arithmetic  2.02 us (1%)
    pallas_call x1, Pallas kernels, device_step(): pl.pallas_call(functools.partial(moe_kernel, (n_tok, hidden, n_exp, ff, c...  140 us

profile of v2, /device:TPU:0, one launch (start us, length us, event | category | flops | bytes accessed | tf_op | source)
XLA Modules:
  0.0 145.9 jit_solution(1707862888275469307)
XLA Ops:
  0.0 0.7 convert_bitcast_fusion
  0.7 1.3 select_maximum_fusion.route
  2.0 1.3 reshape.3.sgate
  3.3 140.3 %shard_map.109 = bf16[256,2048]{1,0:T(8,128)(2,1)} custom-call(bf16[256,2048]{1,0:T(8,128)(2,1)} %tok.1, f32[16,256]{1,0:T(8,128)} %select_maximum_fusion.route, bf16[1,2048]{1,0:T(2,128)(2,1)} %reshape.3.sgate, bf16[2048,2816]{1,0:T(8,128)(2,1)} %sw1.1, bf16[2048,2816]{1,0:T(8,128)(2,1)} %sw3.1, bf16[2816,2048]{1,0:T(8,128)(2,1)} %sw2.1, ...), custom_call_target="tpu_custom_call" | custom-call | tf_op jit(solution)/shard_map/pallas_call | solution.py:332
  143.6 2.3 %copy.13 = bf16[256,2048]{1,0:T(8,128)(2,1)} copy(bf16[256,2048]{1,0:T(8,128)(2,1)} %shard_map.109) | data formatting | bytes 2097152

commit v3 on v0

v3 whole, which is shorter than its diff:
```python
import functools

import jax
import jax.numpy as jnp
from jax import lax
from jax.experimental import pallas as pl
from jax.experimental.pallas import tpu as pltpu
from jax.sharding import PartitionSpec as P

MESH = pl.DeviceIdType.MESH
F32 = jnp.float32
BF16 = jnp.bfloat16
CHUNK = 256
BLOCK = 512
RING = 3
PIECES = 8
GROUP = 4
BATCH = 8
LAG = 2
BF16_MAX = 3.3895313892515355e38


def moe_kernel(cfg, tok, ids, slots, gates, sgate, sw1, sw3, sw2, ew1, ew3, ew2, y,
               toks, ids_v, slots_v, gates_v, sgate_v, rts, wbuf, xg, h, gs, rbuf, sig, acc,
               send3, send1, recv3, recv1, recvu,
               load_sem, wsem, tsem, tok_send, tok_recv, rt_send, rt_recv,
               s3_send, s1_send, su_send, r3_sem, r1_sem, ru_sem):
    n_tok, hidden, n_exp, ff, cap, top_k = cfg
    rows = 4 * cap
    n_chunks = hidden // CHUNK
    offsets = list(range(0, ff, BLOCK))
    widths = [min(BLOCK, ff - o) for o in offsets]
    n_blocks = len(offsets)
    per_place = 2 * (ff // CHUNK)
    n_sub = RING * per_place
    n_tiles = n_chunks * n_exp
    piece = n_tok // PIECES
    slots_all = n_exp * cap

    dp = lax.axis_index('dp')
    me = lax.axis_index('ep')
    partner = (dp, me + 1 - 2 * lax.rem(me, 2))
    across = (dp, lax.rem(me + 2, 4))
    diagonal = (dp, 3 - me)

    def block_copies(n, srcs, b):
        place = n % RING if isinstance(n, int) else lax.rem(n, RING)
        col = pl.ds(offsets[b], widths[b])
        return [pltpu.make_async_copy(src, wbuf.at[place, i, :, col], wsem.at[place, i, b]) for i, src in enumerate(srcs)]

    def shared_block(half, b):
        col = pl.ds(half * ff + offsets[b], widths[b])
        return block_copies(half, (sw1.at[:, col], sw3.at[:, col]), b)

    def expert_block(exp, b):
        col = pl.ds(offsets[b], widths[b])
        return block_copies(exp + 2, (ew1.at[exp, :, col], ew3.at[exp, :, col]), b)

    def start(copies):
        for copy in copies:
            copy.start()

    def wait(copies):
        for copy in copies:
            copy.wait()

    def tiles_in(b):
        return range(offsets[b] // CHUNK * 2, (offsets[b] + widths[b]) // CHUNK * 2)

    def start_after(exp, b):
        @pl.when(exp + RING < n_exp)
        def _():
            start(expert_block(exp + RING, b))

        @pl.when(exp + RING >= n_exp)
        def _():
            for t in tiles_in(b):
                start_tile((exp + RING - n_exp) * per_place + t)

    def tile_place(tile):
        sub = lax.rem(tile, n_sub)
        place = lax.rem(n_exp + 2 + sub // per_place, RING)
        r = lax.rem(sub, per_place)
        lane = pl.multiple_of(r // 2 * CHUNK, CHUNK)
        return (place, lax.rem(r, 2), pl.ds(0, ff), pl.ds(lane, CHUNK)), sub

    def tile_copy(tile):
        where, sub = tile_place(tile)
        chunk, exp = tile // n_exp, lax.rem(tile, n_exp)
        col = pl.ds(pl.multiple_of(chunk * CHUNK, CHUNK), CHUNK)
        return pltpu.make_async_copy(ew2.at[exp, :, col], wbuf.at[where], tsem.at[sub])

    def start_tile(tile):
        tile_copy(tile).start()

    def next_tile(tile):
        @pl.when(tile + n_sub < n_tiles)
        def _():
            start_tile(tile + n_sub)

    n_held = (n_exp * rows // ff) * (ff // CHUNK)

    def shared_place(tile):
        if tile < n_held:
            row, lane = divmod(tile, ff // CHUNK)
            return h.at[pl.ds(row * ff, ff), pl.ds(lane * CHUNK, CHUNK)]
        lane, which = divmod(tile - n_held, 2)
        return wbuf.at[0, which, pl.ds(0, ff), pl.ds(lane * CHUNK, CHUNK)]

    def shared_tile(tile):
        chunk, half = divmod(tile, 2)
        return pltpu.make_async_copy(sw2.at[pl.ds(half * ff, ff), pl.ds(chunk * CHUNK, CHUNK)],
                                     shared_place(tile), tsem.at[tile])

    def remote(src, dst, send, recv, peer):
        return pltpu.make_async_remote_copy(src_ref=src, dst_ref=dst, send_sem=send, recv_sem=recv,
                                            device_id=peer, device_id_type=MESH)

    loads = [pltpu.make_async_copy(src, dst, load_sem.at[i]) for i, (src, dst) in enumerate(
        ((ids, ids_v), (slots, slots_v), (gates, gates_v), (sgate, sgate_v), (tok, toks.at[0])))]
    start(loads)
    barrier = pltpu.get_barrier_semaphore()
    for peer in (partner, across, diagonal):
        pl.semaphore_signal(barrier, inc=1, device_id=peer, device_id_type=MESH)
    with jax.named_scope('own_load'):
        wait(loads)
    start(shared_block(0, 0))
    dest = jnp.where(slots_v[...] >= 0, ids_v[...] * cap + slots_v[...], -1).astype(F32)
    rts[0] = jnp.zeros_like(rts[0])
    rts[0, 0:top_k, :] = dest
    rts[0, 8:8 + top_k, :] = gates_v[...]
    with jax.named_scope('barrier'):
        pl.semaphore_wait(barrier, 3)

    def piece_of(ref, i):
        return ref.at[pl.ds(i * piece, piece)]

    tok_across = [remote(piece_of(toks.at[0], i), piece_of(toks.at[2], i), tok_send.at[i], tok_recv.at[i], across)
                  for i in range(PIECES)]
    tok_partner = remote(toks.at[0], toks.at[1], tok_send.at[2 * PIECES], tok_recv.at[2 * PIECES], partner)
    rt_copies = [remote(rts.at[0], rts.at[d], rt_send.at[d], rt_recv.at[d], peer)
                 for d, peer in ((1, partner), (2, across), (3, diagonal))]
    start(rt_copies + tok_across + [tok_partner])
    for half in range(2):
        for b in range(n_blocks):
            if (half, b) != (0, 0):
                start(shared_block(half, b))
    for tile in range(n_held):
        shared_tile(tile).start()
    for b in range(n_blocks):
        start(expert_block(0, b))
    tok_relay = [remote(piece_of(toks.at[2], i), piece_of(toks.at[3], i), tok_send.at[PIECES + i],
                        tok_recv.at[PIECES + i], partner) for i in range(PIECES)]

    def relay(begin, end):
        for i in range(begin, end):
            tok_across[i].wait_recv()
            tok_relay[i].start()

    def swiglu_block(x, place, b, store):
        done = 0
        while done < widths[b]:
            width = min(CHUNK, widths[b] - done)
            if width == CHUNK:
                a = jnp.dot(x(), wbuf[place, 0, :, pl.ds(offsets[b] + done, width)], preferred_element_type=F32)
                g = jnp.dot(x(), wbuf[place, 1, :, pl.ds(offsets[b] + done, width)], preferred_element_type=F32)
            else:
                w = jnp.concatenate([wbuf[place, 0, :, pl.ds(offsets[b] + done, width)], wbuf[place, 1, :, pl.ds(offsets[b] + done, width)]], axis=1)
                both = jnp.dot(x(), w, preferred_element_type=F32)
                a, g = both[:, :width], both[:, width:]
            store(offsets[b] + done, width, (jax.nn.silu(a) * g).astype(BF16))
            done += width

    with jax.named_scope('shared'):
        for half in range(2):
            for b in range(n_blocks):
                wait(shared_block(half, b))

                def store_shared(col, width, value):
                    xg[pl.ds(half * n_tok, n_tok), pl.ds(col, width)] = value

                swiglu_block(lambda: toks[0], half, b, store_shared)
                if half == 0:
                    for t in tiles_in(b):
                        if n_held + t < 2 * n_chunks:
                            shared_tile(n_held + t).start()

    total = jnp.zeros((n_tok, 128), F32)
    for i in range(hidden // 128):
        total += toks[0, :, pl.ds(i * 128, 128)].astype(F32) * sgate_v[i:i + 1, :].astype(F32)
    logit = jnp.sum(total, axis=1, keepdims=True)
    sig[...] = jnp.broadcast_to(jax.nn.sigmoid(logit), sig.shape)

    with jax.named_scope('shared2'):
        for tile in range(2 * n_chunks):
            shared_tile(tile).wait()
        for chunk in range(n_chunks):
            s = sum(jnp.dot(xg[pl.ds(half * n_tok, n_tok), pl.ds(0, ff)], shared_place(2 * chunk + half)[...],
                            preferred_element_type=F32) for half in range(2))
            acc[chunk] = toks[0, :, pl.ds(chunk * CHUNK, CHUNK)].astype(F32) + sig[:, 0:1] * s
        for exp in range(1, RING):
            for b in range(n_blocks):
                start(expert_block(exp, b))

    relay(0, PIECES // 2)
    with jax.named_scope('wait_near'):
        for copy in rt_copies:
            copy.wait_recv()
        tok_partner.wait_recv()
    base = (me * slots_all).astype(F32)

    with jax.named_scope('weights'):
        for d in range(4):
            def weight_block(i, carry):
                row = (lax.broadcasted_iota(jnp.int32, (128, n_tok), 0) + i * 128).astype(F32) + base
                g = jnp.zeros((128, n_tok), F32)
                for k in range(top_k):
                    g += jnp.where(row == rts[d, k:k + 1, :], rts[d, 8 + k:9 + k, :], 0.0)
                g = g.T
                g1 = jnp.minimum(g, BF16_MAX).astype(BF16)
                left = g - g1.astype(F32)
                g2 = left.astype(BF16)
                g3 = (left - g2.astype(F32)).astype(BF16)
                for part, value in enumerate((g1, g2, g3)):
                    gs[d, :, pl.ds(pl.multiple_of(part * slots_all + i * 128, 128), 128)] = value
                return carry
            lax.fori_loop(0, slots_all // 128, weight_block, 0)

    def gather(g, sources):
        for d in sources:
            row = (lax.broadcasted_iota(jnp.int32, (GROUP * cap, n_tok), 0) + g * (GROUP * cap)).astype(F32) + base
            pick = jnp.zeros((GROUP * cap, n_tok), F32)
            for k in range(top_k):
                pick += jnp.where(row == rts[d, k:k + 1, :], 1.0, 0.0)
            pick = pick.astype(BF16)
            for i in range(hidden // 512):
                col = pl.ds(i * 512, 512)
                got = jnp.dot(pick, toks[d, :, col], preferred_element_type=F32).astype(BF16)
                for e in range(GROUP):
                    xg[pl.ds(e * rows + d * cap, cap), col] = got[e * cap:(e + 1) * cap]

    with jax.named_scope('gather_near'):
        gather(jnp.int32(0), (0, 1))
    relay(PIECES // 2, PIECES - 2)

    with jax.named_scope('dispatch_wait'):
        relay(PIECES - 2, PIECES)
        gather(jnp.int32(0), (2,))
        for copy in tok_relay:
            copy.wait_recv()

    def keep_rows(exp, r):
        for d in range(4):
            rbuf[d, pl.ds(pl.multiple_of(exp * cap, 16), cap), :] = r[d * cap:(d + 1) * cap]

    def h_rows(exp):
        return pl.ds(pl.multiple_of(exp * rows, rows), rows)

    def group_step(g, carry):
        with jax.named_scope('gather'):
            @pl.when(g == 0)
            def _():
                gather(g, (3,))

            @pl.when(g > 0)
            def _():
                gather(g, range(4))

        def expert_step(i, carry):
            exp = g * GROUP + i
            x_rows = pl.ds(pl.multiple_of(i * rows, rows), rows)

            def store_h(col, width, value):
                h[h_rows(exp), pl.ds(col, width)] = value

            def block(b):
                swiglu_block(lambda: xg[x_rows, :], lax.rem(exp + 2, RING), b, store_h)

            edge = (exp == 0) | (exp == n_exp - 1)

            @pl.when(edge)
            def _():
                for b in range(n_blocks):
                    with jax.named_scope('edge_wait'):
                        wait(expert_block(exp, b))
                    with jax.named_scope('edge_block'):
                        block(b)
                        start_after(exp, b)

            @pl.when(jnp.logical_not(edge))
            def _():
                with jax.named_scope('w_wait'):
                    for b in range(n_blocks):
                        wait(expert_block(exp, b))
                with jax.named_scope('expert'):
                    for b in range(n_blocks):
                        block(b)
                    for b in range(n_blocks):
                        start_after(exp, b)
            return carry
        lax.fori_loop(0, GROUP, expert_step, 0)
        return carry
    lax.fori_loop(0, n_exp // GROUP, group_step, 0)

    def combine(d):
        r = rbuf[d]
        return jnp.dot(gs[d], jnp.concatenate([r, r, r], axis=0), preferred_element_type=F32)

    def to_partner3(j):
        return remote(send3.at[lax.rem(j, 2)], recv3.at[lax.rem(j, 4)], s3_send.at[lax.rem(j, 2)], r3_sem.at[j], partner)

    def to_partner1(j):
        return remote(send1.at[lax.rem(j, 2)], recv1.at[lax.rem(j, 4)], s1_send.at[lax.rem(j, 2)], r1_sem.at[j], partner)

    def to_across(j):
        return remote(recv3.at[lax.rem(j, 4)], recvu.at[lax.rem(j, 6)], su_send.at[j], ru_sem.at[j], across)

    def finish(j):
        to_partner1(j).wait_recv()
        to_across(j).wait_recv()
        col = pl.ds(pl.multiple_of(j * CHUNK, CHUNK), CHUNK)
        y[:, col] = (acc[j] + recv1[lax.rem(j, 4)] + recvu[lax.rem(j, 6)]).astype(y.dtype)

    def chunk_step(j, carry):
        def batch_step(i, carry):
            tile = j * n_exp + BATCH * i
            with jax.named_scope('t_wait'):
                for u in range(BATCH):
                    tile_copy(tile + u).wait()
            for u in range(BATCH):
                exp = BATCH * i + u
                keep_rows(exp, jnp.dot(h[h_rows(exp), :], wbuf[tile_place(tile + u)[0]],
                                       preferred_element_type=F32).astype(BF16))
            for u in range(BATCH):
                next_tile(tile + u)
            return carry

        with jax.named_scope('tiles'):
            lax.fori_loop(0, n_exp // BATCH, batch_step, 0)

        @pl.when(j >= 3)
        def _():
            with jax.named_scope('su_wait'):
                to_across(j - 3).wait_send()

        @pl.when(j >= 2)
        def _():
            to_partner3(j - 2).wait_send()
            to_partner1(j - 2).wait_send()

        with jax.named_scope('combine3'):
            send3[lax.rem(j, 2)] = combine(3)
            to_partner3(j).start()
        with jax.named_scope('combine120'):
            part2 = combine(2)
            send1[lax.rem(j, 2)] = combine(1)
            acc[j] = acc[j] + combine(0)
            to_partner1(j).start()
        with jax.named_scope('pwait'):
            to_partner3(j).wait_recv()
            recv3[lax.rem(j, 4)] = recv3[lax.rem(j, 4)] + part2
            to_across(j).start()

        @pl.when(j >= LAG)
        def _():
            with jax.named_scope('finish'):
                finish(j - LAG)
        return carry
    lax.fori_loop(0, n_chunks, chunk_step, 0)

    def last_step(j, carry):
        with jax.named_scope('last'):
            finish(j)
        return carry
    lax.fori_loop(n_chunks - LAG, n_chunks, last_step, 0)

    for copy in rt_copies + tok_across + tok_relay + [tok_partner]:
        copy.wait_send()
    for j in range(n_chunks - 2, n_chunks):
        to_partner3(j).wait_send()
        to_partner1(j).wait_send()
    for j in range(n_chunks - 3, n_chunks):
        to_across(j).wait_send()


def solution(mesh):
    num_ep = mesh.shape['ep']
    row_spec = P(('dp', 'ep'), None)
    expert_spec = P('ep', None, None)

    def device_step(tokens, expert_ids, gate_vals, slots, shared_w1, shared_w3, shared_w2, shared_gate, expert_w1, expert_w3, expert_w2):
        n_tok, hidden = tokens.shape
        top_k = expert_ids.shape[1]
        n_exp, _, ff = expert_w1.shape
        num_experts = n_exp * num_ep
        cap = 8 * ((2 * n_tok * top_k + 8 * num_experts - 1) // (8 * num_experts))
        rows = num_ep * cap
        n_chunks = hidden // CHUNK
        n_sub = RING * 2 * (ff // CHUNK)
        n_blocks = -(-ff // BLOCK)

        anywhere = pl.BlockSpec(memory_space=pl.ANY)
        dma = pltpu.SemaphoreType.DMA
        vm = pltpu.VMEM
        block = (n_tok, CHUNK)
        return pl.pallas_call(
            functools.partial(moe_kernel, (n_tok, hidden, n_exp, ff, cap, top_k)),
            out_shape=jax.ShapeDtypeStruct((n_tok, hidden), tokens.dtype),
            in_specs=[anywhere] * 11,
            out_specs=pl.BlockSpec(memory_space=pltpu.VMEM),
            scratch_shapes=[
                vm((4, n_tok, hidden), BF16),
                vm((top_k, n_tok), jnp.int32), vm((top_k, n_tok), jnp.int32), vm((top_k, n_tok), F32),
                vm((hidden // 128, 128), BF16),
                vm((4, 16, n_tok), F32),
                vm((RING, 2, hidden, ff), BF16),
                vm((GROUP * rows, hidden), BF16),
                vm((n_exp * rows, ff), BF16),
                vm((4, n_tok, 3 * n_exp * cap), BF16),
                vm((4, n_exp * cap, CHUNK), BF16),
                vm((n_tok, 128), F32),
                vm((n_chunks,) + block, F32),
                vm((2,) + block, F32), vm((2,) + block, F32),
                vm((4,) + block, F32), vm((4,) + block, F32), vm((6,) + block, F32),
                dma((5,)), dma((RING, 2, n_blocks)), dma((n_sub,)),
                dma((2 * PIECES + 1,)), dma((2 * PIECES + 1,)), dma((4,)), dma((4,)),
                dma((2,)), dma((2,)), dma((n_chunks,)),
                dma((n_chunks,)), dma((n_chunks,)), dma((n_chunks,)),
            ],
            compiler_params=pltpu.CompilerParams(collective_id=0, has_side_effects=True, vmem_limit_bytes=67043328),
        )(tokens, expert_ids.T, slots.T, gate_vals.T, shared_gate.reshape(hidden // 128, 128),
          shared_w1, shared_w3, shared_w2, expert_w1, expert_w3, expert_w2)

    return jax.shard_map(device_step, mesh=mesh, in_specs=(row_spec, row_spec, row_spec, row_spec, P(), P(), P(), P(), expert_spec, expert_spec, expert_spec), out_specs=row_spec, check_vma=False)
```

time: 519 us -> 138 us (0.27)
  matrix products: 150 us -> 0 us
  blocking collectives: 143 us -> 0 us
  Pallas kernels: 0 us -> 135 us
  waiting for transfers between devices: 127 us -> 0 us
  local copies, waits for them, and re-layouts: 72.9 us -> 2.3 us
  other arithmetic: 18.2 us -> 0 us
  starting transfers between devices: 6.64 us -> 0 us
    dot_general x6 -> x0, matrix products: 150 us -> none  [the longest x1 46.1 us: device_step(): jnp.einsum('secd,edf->secf', expert_in, expert_w1, preferred_element_type...]
    all_to_all x1 -> x0, blocking collectives: 143 us -> none  [device_step(): lax.all_to_all(send_buf.reshape(num_ep, local_experts * capacity, hidden)...]
    pallas_call x0 -> x1, Pallas kernels: none -> 135 us  [device_step(): pl.pallas_call(functools.partial(moe_kernel, (n_tok, hidden, n_exp, ff, c...]
    all_to_all x1 -> x0, waiting for transfers between devices: 127 us -> none  [device_step(): lax.all_to_all(expert_out.reshape(num_ep, local_experts * capacity, hidde...]
    gather x3 -> x0, local copies, waits for them, and re-layouts: 55.1 us -> none  [the longest x2 29.9 us: device_step(): jnp.take(back_buf.reshape(buf_rows, hidden), slot_dest, axis=0, mode='fil...]
    convert_element_type x1 -> x0, local copies, waits for them, and re-layouts: 10.7 us -> none  [device_step(): jnp.einsum('secf,efd->secd', hidden_act, expert_w2, preferred_element_typ...]
    reduce_sum x1 -> x0, other arithmetic: 10.5 us -> none  [device_step(): routed = jnp.sum(weights * picked, axis=1)]
    all_to_all x1 -> x0, starting transfers between devices: 6.64 us -> none  [device_step(): lax.all_to_all(expert_out.reshape(num_ep, local_experts * capacity, hidde...]
  transfers between devices with their start and end apart: 1 -> 0, of which waited for: 1 -> 0; matrix products, arithmetic and copies ran while one was open for 2% -> 0% of each run, Pallas kernels for 0% -> 0%
where the time goes in v3:
time: 138 us; the launch traced here: 137 us
  Pallas kernels  135 us (98%)
  local copies, waits for them, and re-layouts  2.3 us (2%)
    pallas_call x1, Pallas kernels, device_step(): pl.pallas_call(functools.partial(moe_kernel, (n_tok, hidden, n_exp, ff, c...  135 us

profile of v3, /device:TPU:0, one launch (start us, length us, event | category | flops | bytes accessed | tf_op | source)
XLA Modules:
  0.0 137.3 jit_solution(2774276374312082914)
XLA Ops:
  0.0 135.0 %shard_map.109 = bf16[256,2048]{1,0:T(8,128)(2,1)} custom-call(bf16[256,2048]{1,0:T(8,128)(2,1)} %tok.1, s32[6,256]{1,0:T(8,128)} %bitcast.4, s32[6,256]{1,0:T(8,128)} %bitcast.5, f32[6,256]{1,0:T(8,128)} %bitcast.6, bf16[16,128]{1,0:T(8,128)(2,1)} %bitcast.7, bf16[2048,2816]{1,0:T(8,128)(2,1)} %sw1.1, bf16[2048,2816]{1,0:T(8,128)(2,1)} %sw3.1, ...), custom_call_target="tpu_custom_call" | custom-call | tf_op jit(solution)/shard_map/pallas_call | solution.py:406
  135.0 2.3 %copy.13 = bf16[256,2048]{1,0:T(8,128)(2,1)} copy(bf16[256,2048]{1,0:T(8,128)(2,1)} %shard_map.109) | data formatting | bytes 2097152

commit v4 on v3

--- a/solution.py
+++ b/solution.py
@@ -21,9 +21,9 @@
 
 
 def moe_kernel(cfg, tok, ids, slots, gates, sgate, sw1, sw3, sw2, ew1, ew3, ew2, y,
-               toks, ids_v, slots_v, gates_v, sgate_v, rts, wbuf, xg, h, gs, rbuf, sig, acc,
+               toks, ids_v, slots_v, gates_v, sgate_v, rts, wbuf, wtail, xg, h, gs, rbuf, sig, acc,
                send3, send1, recv3, recv1, recvu,
-               load_sem, wsem, tsem, tok_send, tok_recv, rt_send, rt_recv,
+               load_sem, wsem, early_sem, tsem, tok_send, tok_recv, rt_send, rt_recv,
                s3_send, s1_send, su_send, r3_sem, r1_sem, ru_sem):
     n_tok, hidden, n_exp, ff, cap, top_k = cfg
     rows = 4 * cap
@@ -32,8 +32,8 @@
     widths = [min(BLOCK, ff - o) for o in offsets]
     n_blocks = len(offsets)
     per_place = 2 * (ff // CHUNK)
-    n_sub = RING * per_place
-    n_tiles = n_chunks * n_exp
+    n_ring = RING * per_place
+    n_sub = 2 * n_exp
     piece = n_tok // PIECES
     slots_all = n_exp * cap
 
@@ -43,18 +43,18 @@
     across = (dp, lax.rem(me + 2, 4))
     diagonal = (dp, 3 - me)
 
-    def block_copies(n, srcs, b):
+    def block_copies(n, srcs, b, which):
         place = n % RING if isinstance(n, int) else lax.rem(n, RING)
         col = pl.ds(offsets[b], widths[b])
-        return [pltpu.make_async_copy(src, wbuf.at[place, i, :, col], wsem.at[place, i, b]) for i, src in enumerate(srcs)]
+        return [pltpu.make_async_copy(srcs[i], wbuf.at[place, i, :, col], wsem.at[place, i, b]) for i in which]
 
     def shared_block(half, b):
         col = pl.ds(half * ff + offsets[b], widths[b])
-        return block_copies(half, (sw1.at[:, col], sw3.at[:, col]), b)
-
-    def expert_block(exp, b):
+        return block_copies(half, (sw1.at[:, col], sw3.at[:, col]), b, (0, 1))
+
+    def expert_block(exp, b, which=(0, 1)):
         col = pl.ds(offsets[b], widths[b])
-        return block_copies(exp + 2, (ew1.at[exp, :, col], ew3.at[exp, :, col]), b)
+        return block_copies(exp + 2, (ew1.at[exp, :, col], ew3.at[exp, :, col]), b, which)
 
     def start(copies):
         for copy in copies:
@@ -72,31 +72,30 @@
         def _():
             start(expert_block(exp + RING, b))
 
-        @pl.when(exp + RING >= n_exp)
-        def _():
-            for t in tiles_in(b):
-                start_tile((exp + RING - n_exp) * per_place + t)
-
-    def tile_place(tile):
-        sub = lax.rem(tile, n_sub)
-        place = lax.rem(n_exp + 2 + sub // per_place, RING)
-        r = lax.rem(sub, per_place)
-        lane = pl.multiple_of(r // 2 * CHUNK, CHUNK)
-        return (place, lax.rem(r, 2), pl.ds(0, ff), pl.ds(lane, CHUNK)), sub
-
-    def tile_copy(tile):
-        where, sub = tile_place(tile)
-        chunk, exp = tile // n_exp, lax.rem(tile, n_exp)
+        for later in range(RING):
+            @pl.when(exp == n_exp - RING + later)
+            def _():
+                for t in tiles_in(b):
+                    start_tile(later * per_place + t)
+
+    early_rows = pl.ds(n_exp * rows - hidden, hidden)
+
+    def early_block(b):
+        col = pl.ds(offsets[b], widths[b])
+        return pltpu.make_async_copy(ew1.at[RING, :, col], h.at[early_rows, col], early_sem.at[b])
+
+    def tile_place(sub):
+        if sub >= n_ring:
+            return wtail.at[sub - n_ring]
+        place, r = divmod(sub, per_place)
+        return wbuf.at[(n_exp + 2 + place) % RING, r % 2, pl.ds(0, ff), pl.ds(r // 2 * CHUNK, CHUNK)]
+
+    def tile_copy(sub, chunk):
         col = pl.ds(pl.multiple_of(chunk * CHUNK, CHUNK), CHUNK)
-        return pltpu.make_async_copy(ew2.at[exp, :, col], wbuf.at[where], tsem.at[sub])
-
-    def start_tile(tile):
-        tile_copy(tile).start()
-
-    def next_tile(tile):
-        @pl.when(tile + n_sub < n_tiles)
-        def _():
-            start_tile(tile + n_sub)
+        return pltpu.make_async_copy(ew2.at[sub % n_exp, :, col], tile_place(sub), tsem.at[sub])
+
+    def start_tile(sub):
+        tile_copy(sub, sub // n_exp).start()
 
     n_held = (n_exp * rows // ff) * (ff // CHUNK)
 
@@ -157,15 +156,15 @@
             tok_across[i].wait_recv()
             tok_relay[i].start()
 
-    def swiglu_block(x, place, b, store):
+    def swiglu_block(x, w1, w3, b, store):
         done = 0
         while done < widths[b]:
             width = min(CHUNK, widths[b] - done)
             if width == CHUNK:
-                a = jnp.dot(x(), wbuf[place, 0, :, pl.ds(offsets[b] + done, width)], preferred_element_type=F32)
-                g = jnp.dot(x(), wbuf[place, 1, :, pl.ds(offsets[b] + done, width)], preferred_element_type=F32)
+                a = jnp.dot(x(), w1[:, pl.ds(offsets[b] + done, width)], preferred_element_type=F32)
+                g = jnp.dot(x(), w3[:, pl.ds(offsets[b] + done, width)], preferred_element_type=F32)
             else:
-                w = jnp.concatenate([wbuf[place, 0, :, pl.ds(offsets[b] + done, width)], wbuf[place, 1, :, pl.ds(offsets[b] + done, width)]], axis=1)
+                w = jnp.concatenate([w1[:, pl.ds(offsets[b] + done, width)], w3[:, pl.ds(offsets[b] + done, width)]], axis=1)
                 both = jnp.dot(x(), w, preferred_element_type=F32)
                 a, g = both[:, :width], both[:, width:]
             store(offsets[b] + done, width, (jax.nn.silu(a) * g).astype(BF16))
@@ -179,7 +178,7 @@
                 def store_shared(col, width, value):
                     xg[pl.ds(half * n_tok, n_tok), pl.ds(col, width)] = value
 
-                swiglu_block(lambda: toks[0], half, b, store_shared)
+                swiglu_block(lambda: toks[0], wbuf.at[half, 0], wbuf.at[half, 1], b, store_shared)
                 if half == 0:
                     for t in tiles_in(b):
                         if n_held + t < 2 * n_chunks:
@@ -192,15 +191,18 @@
     sig[...] = jnp.broadcast_to(jax.nn.sigmoid(logit), sig.shape)
 
     with jax.named_scope('shared2'):
-        for tile in range(2 * n_chunks):
-            shared_tile(tile).wait()
+        for b in range(n_blocks):
+            start(expert_block(2, b))
         for chunk in range(n_chunks):
+            for half in range(2):
+                shared_tile(2 * chunk + half).wait()
             s = sum(jnp.dot(xg[pl.ds(half * n_tok, n_tok), pl.ds(0, ff)], shared_place(2 * chunk + half)[...],
                             preferred_element_type=F32) for half in range(2))
             acc[chunk] = toks[0, :, pl.ds(chunk * CHUNK, CHUNK)].astype(F32) + sig[:, 0:1] * s
-        for exp in range(1, RING):
-            for b in range(n_blocks):
-                start(expert_block(exp, b))
+        for b in range(n_blocks):
+            start(expert_block(1, b))
+        for b in range(n_blocks):
+            early_block(b).start()
 
     relay(0, PIECES // 2)
     with jax.named_scope('wait_near'):
@@ -249,12 +251,8 @@
         for copy in tok_relay:
             copy.wait_recv()
 
-    def keep_rows(exp, r):
-        for d in range(4):
-            rbuf[d, pl.ds(pl.multiple_of(exp * cap, 16), cap), :] = r[d * cap:(d + 1) * cap]
-
     def h_rows(exp):
-        return pl.ds(pl.multiple_of(exp * rows, rows), rows)
+        return pl.ds(exp * rows if isinstance(exp, int) else pl.multiple_of(exp * rows, rows), rows)
 
     def group_step(g, carry):
         with jax.named_scope('gather'):
@@ -268,49 +266,64 @@
 
         def expert_step(i, carry):
             exp = g * GROUP + i
-            x_rows = pl.ds(pl.multiple_of(i * rows, rows), rows)
-
-            def store_h(col, width, value):
-                h[h_rows(exp), pl.ds(col, width)] = value
-
-            def block(b):
-                swiglu_block(lambda: xg[x_rows, :], lax.rem(exp + 2, RING), b, store_h)
-
-            edge = (exp == 0) | (exp == n_exp - 1)
-
-            @pl.when(edge)
-            def _():
+            place = lax.rem(exp + 2, RING)
+
+            def whole(e, slot, w1):
+                x_rows = pl.ds(pl.multiple_of(i * rows, rows), rows)
+
+                def store_h(col, width, value):
+                    h[h_rows(e), pl.ds(col, width)] = value
+
                 for b in range(n_blocks):
-                    with jax.named_scope('edge_wait'):
-                        wait(expert_block(exp, b))
-                    with jax.named_scope('edge_block'):
-                        block(b)
-                        start_after(exp, b)
-
-            @pl.when(jnp.logical_not(edge))
+                    swiglu_block(lambda: xg[x_rows, :], w1, wbuf.at[slot, 1], b, store_h)
+
+            @pl.when(exp == RING)
+            def _():
+                with jax.named_scope('early_wait'):
+                    for b in range(n_blocks):
+                        early_block(b).wait()
+                        wait(expert_block(exp, b, (1,)))
+                with jax.named_scope('early'):
+                    whole(RING, (RING + 2) % RING, h.at[early_rows])
+                    for b in range(n_blocks):
+                        start(expert_block(exp + RING, b, (1,)))
+
+            @pl.when(exp != RING)
             def _():
                 with jax.named_scope('w_wait'):
                     for b in range(n_blocks):
                         wait(expert_block(exp, b))
                 with jax.named_scope('expert'):
-                    for b in range(n_blocks):
-                        block(b)
-                    for b in range(n_blocks):
-                        start_after(exp, b)
+                    whole(exp, place, wbuf.at[place, 0])
+
+                    @pl.when(exp == 0)
+                    def _():
+                        for b in range(n_blocks):
+                            start(expert_block(exp + RING, b, (1,)))
+                        for b in range(n_blocks):
+                            start(expert_block(exp + 2 * RING, b, (0,)))
+
+                    @pl.when(exp > 0)
+                    def _():
+                        for b in range(n_blocks):
+                            start_after(exp, b)
             return carry
         lax.fori_loop(0, GROUP, expert_step, 0)
         return carry
     lax.fori_loop(0, n_exp // GROUP, group_step, 0)
 
+    for sub in range(n_ring, n_sub):
+        start_tile(sub)
+
     def combine(d):
         r = rbuf[d]
         return jnp.dot(gs[d], jnp.concatenate([r, r, r], axis=0), preferred_element_type=F32)
 
     def to_partner3(j):
-        return remote(send3.at[lax.rem(j, 2)], recv3.at[lax.rem(j, 4)], s3_send.at[lax.rem(j, 2)], r3_sem.at[j], partner)
+        return remote(send3, recv3.at[lax.rem(j, 4)], s3_send, r3_sem.at[j], partner)
 
     def to_partner1(j):
-        return remote(send1.at[lax.rem(j, 2)], recv1.at[lax.rem(j, 4)], s1_send.at[lax.rem(j, 2)], r1_sem.at[j], partner)
+        return remote(send1, recv1.at[lax.rem(j, 4)], s1_send, r1_sem.at[j], partner)
 
     def to_across(j):
         return remote(recv3.at[lax.rem(j, 4)], recvu.at[lax.rem(j, 6)], su_send.at[j], ru_sem.at[j], across)
@@ -321,39 +334,39 @@
         col = pl.ds(pl.multiple_of(j * CHUNK, CHUNK), CHUNK)
         y[:, col] = (acc[j] + recv1[lax.rem(j, 4)] + recvu[lax.rem(j, 6)]).astype(y.dtype)
 
-    def chunk_step(j, carry):
-        def batch_step(i, carry):
-            tile = j * n_exp + BATCH * i
+    def chunk_step(j, first):
+        for begin in range(0, n_exp, BATCH):
+            batch = range(begin, begin + BATCH)
             with jax.named_scope('t_wait'):
-                for u in range(BATCH):
-                    tile_copy(tile + u).wait()
-            for u in range(BATCH):
-                exp = BATCH * i + u
-                keep_rows(exp, jnp.dot(h[h_rows(exp), :], wbuf[tile_place(tile + u)[0]],
-                                       preferred_element_type=F32).astype(BF16))
-            for u in range(BATCH):
-                next_tile(tile + u)
-            return carry
-
-        with jax.named_scope('tiles'):
-            lax.fori_loop(0, n_exp // BATCH, batch_step, 0)
+                for exp in batch:
+                    tile_copy(first + exp, j).wait()
+            with jax.named_scope('tiles'):
+                for exp in batch:
+                    r = jnp.dot(h[pl.ds(exp * rows, rows), :], tile_place(first + exp)[...], preferred_element_type=F32).astype(BF16)
+                    for d in range(4):
+                        rbuf[d, pl.ds(exp * cap, cap), :] = r[d * cap:(d + 1) * cap]
+
+            @pl.when(j + 2 < n_chunks)
+            def _():
+                for exp in batch:
+                    tile_copy(first + exp, j + 2).start()
 
         @pl.when(j >= 3)
         def _():
             with jax.named_scope('su_wait'):
                 to_across(j - 3).wait_send()
 
-        @pl.when(j >= 2)
+        @pl.when(j >= 1)
         def _():
-            to_partner3(j - 2).wait_send()
-            to_partner1(j - 2).wait_send()
+            to_partner3(j - 1).wait_send()
+            to_partner1(j - 1).wait_send()
 
         with jax.named_scope('combine3'):
-            send3[lax.rem(j, 2)] = combine(3)
+            send3[...] = combine(3)
             to_partner3(j).start()
-        with jax.named_scope('combine120'):
+        with jax.named_scope('combine210'):
             part2 = combine(2)
-            send1[lax.rem(j, 2)] = combine(1)
+            send1[...] = combine(1)
             acc[j] = acc[j] + combine(0)
             to_partner1(j).start()
         with jax.named_scope('pwait'):
@@ -365,8 +378,12 @@
         def _():
             with jax.named_scope('finish'):
                 finish(j - LAG)
+
+    def two_chunks(i, carry):
+        chunk_step(2 * i, 0)
+        chunk_step(2 * i + 1, n_exp)
         return carry
-    lax.fori_loop(0, n_chunks, chunk_step, 0)
+    lax.fori_loop(0, n_chunks // 2, two_chunks, 0)
 
     def last_step(j, carry):
         with jax.named_scope('last'):
@@ -376,9 +393,8 @@
 
     for copy in rt_copies + tok_across + tok_relay + [tok_partner]:
         copy.wait_send()
-    for j in range(n_chunks - 2, n_chunks):
-        to_partner3(j).wait_send()
-        to_partner1(j).wait_send()
+    to_partner3(n_chunks - 1).wait_send()
+    to_partner1(n_chunks - 1).wait_send()
     for j in range(n_chunks - 3, n_chunks):
         to_across(j).wait_send()
 
@@ -396,7 +412,8 @@
         cap = 8 * ((2 * n_tok * top_k + 8 * num_experts - 1) // (8 * num_experts))
         rows = num_ep * cap
         n_chunks = hidden // CHUNK
-        n_sub = RING * 2 * (ff // CHUNK)
+        n_sub = 2 * n_exp
+        n_tail = n_sub - RING * 2 * (ff // CHUNK)
         n_blocks = -(-ff // BLOCK)
 
         anywhere = pl.BlockSpec(memory_space=pl.ANY)
@@ -405,7 +422,7 @@
         block = (n_tok, CHUNK)
         return pl.pallas_call(
             functools.partial(moe_kernel, (n_tok, hidden, n_exp, ff, cap, top_k)),
-            out_shape=jax.ShapeDtypeStruct((n_tok, hidden), tokens.dtype),
+            out_shape=pltpu.VMEM((n_tok, hidden), tokens.dtype),
             in_specs=[anywhere] * 11,
             out_specs=pl.BlockSpec(memory_space=pltpu.VMEM),
             scratch_shapes=[
@@ -414,20 +431,21 @@
                 vm((hidden // 128, 128), BF16),
                 vm((4, 16, n_tok), F32),
                 vm((RING, 2, hidden, ff), BF16),
+                vm((n_tail, ff, CHUNK), BF16),
                 vm((GROUP * rows, hidden), BF16),
                 vm((n_exp * rows, ff), BF16),
                 vm((4, n_tok, 3 * n_exp * cap), BF16),
                 vm((4, n_exp * cap, CHUNK), BF16),
                 vm((n_tok, 128), F32),
                 vm((n_chunks,) + block, F32),
-                vm((2,) + block, F32), vm((2,) + block, F32),
+                vm(block, F32), vm(block, F32),
                 vm((4,) + block, F32), vm((4,) + block, F32), vm((6,) + block, F32),
-                dma((5,)), dma((RING, 2, n_blocks)), dma((n_sub,)),
+                dma((5,)), dma((RING, 2, n_blocks)), dma((n_blocks,)), dma((n_sub,)),
                 dma((2 * PIECES + 1,)), dma((2 * PIECES + 1,)), dma((4,)), dma((4,)),
-                dma((2,)), dma((2,)), dma((n_chunks,)),
+                dma, dma, dma((n_chunks,)),
                 dma((n_chunks,)), dma((n_chunks,)), dma((n_chunks,)),
             ],
-            compiler_params=pltpu.CompilerParams(collective_id=0, has_side_effects=True, vmem_limit_bytes=67043328),
+            compiler_params=pltpu.CompilerParams(collective_id=0, has_side_effects=True, vmem_limit_bytes=65994752),
         )(tokens, expert_ids.T, slots.T, gate_vals.T, shared_gate.reshape(hidden // 128, 128),
           shared_w1, shared_w3, shared_w2, expert_w1, expert_w3, expert_w2)
 

time: 138 us -> 133 us (0.964)
  Pallas kernels: 135 us -> 132 us
    pallas_call x1, Pallas kernels: 135 us -> 132 us  [device_step(): pl.pallas_call(functools.partial(moe_kernel, (n_tok, hidden, n_exp, ff, c...]
where the time goes in v4:
time: 133 us
  Pallas kernels  132 us (99%)
    pallas_call x1, Pallas kernels, device_step(): pl.pallas_call(functools.partial(moe_kernel, (n_tok, hidden, n_exp, ff, c...  132 us

profile of v4, /device:TPU:0, one launch (start us, length us, event | category | flops | bytes accessed | tf_op | source)
XLA Modules:
  0.0 133.0 jit_solution(4193863753415716944)
XLA Ops:
  0.0 132.0 %shard_map.109 = bf16[256,2048]{1,0:T(8,128)(2,1)S(1)} custom-call(bf16[256,2048]{1,0:T(8,128)(2,1)} %tok.1, s32[6,256]{1,0:T(8,128)} %bitcast.4, s32[6,256]{1,0:T(8,128)} %bitcast.5, f32[6,256]{1,0:T(8,128)} %bitcast.6, bf16[16,128]{1,0:T(8,128)(2,1)} %bitcast.7, bf16[2048,2816]{1,0:T(8,128)(2,1)} %sw1.1, bf16[2048,2816]{1,0:T(8,128)(2,1)} %sw3.1, ...), custom_call_target="tpu_custom_call" | custom-call | tf_op jit(solution)/shard_map/pallas_call | solution.py:423
  132.0 1.0 copy.13

commit v5 on v4

--- a/solution.py
+++ b/solution.py
@@ -72,7 +72,7 @@
         def _():
             start(expert_block(exp + RING, b))
 
-        for later in range(RING):
+        for later in range(RING - 1):
             @pl.when(exp == n_exp - RING + later)
             def _():
                 for t in tiles_in(b):
@@ -115,15 +115,19 @@
         return pltpu.make_async_remote_copy(src_ref=src, dst_ref=dst, send_sem=send, recv_sem=recv,
                                             device_id=peer, device_id_type=MESH)
 
-    loads = [pltpu.make_async_copy(src, dst, load_sem.at[i]) for i, (src, dst) in enumerate(
-        ((ids, ids_v), (slots, slots_v), (gates, gates_v), (sgate, sgate_v), (tok, toks.at[0])))]
-    start(loads)
+    def piece_of(ref, i):
+        return ref.at[pl.ds(i * piece, piece)]
+
     barrier = pltpu.get_barrier_semaphore()
     for peer in (partner, across, diagonal):
         pl.semaphore_signal(barrier, inc=1, device_id=peer, device_id_type=MESH)
+    tok_loads = [pltpu.make_async_copy(piece_of(tok, i), piece_of(toks.at[0], i), load_sem.at[i]) for i in range(PIECES)]
+    loads = [pltpu.make_async_copy(src, dst, load_sem.at[PIECES + i]) for i, (src, dst) in enumerate(
+        ((ids, ids_v), (slots, slots_v), (gates, gates_v), (sgate, sgate_v)))]
+    start(loads + tok_loads)
+    start(shared_block(0, 0))
     with jax.named_scope('own_load'):
         wait(loads)
-    start(shared_block(0, 0))
     dest = jnp.where(slots_v[...] >= 0, ids_v[...] * cap + slots_v[...], -1).astype(F32)
     rts[0] = jnp.zeros_like(rts[0])
     rts[0, 0:top_k, :] = dest
@@ -131,15 +135,16 @@
     with jax.named_scope('barrier'):
         pl.semaphore_wait(barrier, 3)
 
-    def piece_of(ref, i):
-        return ref.at[pl.ds(i * piece, piece)]
-
     tok_across = [remote(piece_of(toks.at[0], i), piece_of(toks.at[2], i), tok_send.at[i], tok_recv.at[i], across)
                   for i in range(PIECES)]
     tok_partner = remote(toks.at[0], toks.at[1], tok_send.at[2 * PIECES], tok_recv.at[2 * PIECES], partner)
     rt_copies = [remote(rts.at[0], rts.at[d], rt_send.at[d], rt_recv.at[d], peer)
                  for d, peer in ((1, partner), (2, across), (3, diagonal))]
-    start(rt_copies + tok_across + [tok_partner])
+    start(rt_copies)
+    for load, copy in zip(tok_loads, tok_across):
+        load.wait()
+        copy.start()
+    tok_partner.start()
     for half in range(2):
         for b in range(n_blocks):
             if (half, b) != (0, 0):
@@ -312,9 +317,6 @@
         return carry
     lax.fori_loop(0, n_exp // GROUP, group_step, 0)
 
-    for sub in range(n_ring, n_sub):
-        start_tile(sub)
-
     def combine(d):
         r = rbuf[d]
         return jnp.dot(gs[d], jnp.concatenate([r, r, r], axis=0), preferred_element_type=F32)
@@ -333,6 +335,46 @@
         to_across(j).wait_recv()
         col = pl.ds(pl.multiple_of(j * CHUNK, CHUNK), CHUNK)
         y[:, col] = (acc[j] + recv1[lax.rem(j, 4)] + recvu[lax.rem(j, 6)]).astype(y.dtype)
+
+    def tile_rows(first, experts, sources):
+        begin, count = sources[0] * cap, len(sources) * cap
+        for exp in experts:
+            r = jnp.dot(h[pl.ds(exp * rows + begin, count), :], tile_place(first + exp)[...],
+                        preferred_element_type=F32).astype(BF16)
+            for i, d in enumerate(sources):
+                rbuf[d, pl.ds(exp * cap, cap), :] = r[i * cap:(i + 1) * cap]
+
+    def first_chunk():
+        for begin in range(0, n_exp, BATCH):
+            for exp in range(begin, begin + BATCH):
+                tile_copy(exp, 0).wait()
+            with jax.named_scope('far_tiles'):
+                tile_rows(0, range(begin, begin + BATCH), (2, 3))
+            if begin == 0:
+                for sub in range((RING - 1) * per_place, n_sub):
+                    start_tile(sub)
+        with jax.named_scope('far_combine3'):
+            send3[...] = combine(3)
+            to_partner3(0).start()
+        with jax.named_scope('far_combine2'):
+            part2 = combine(2)
+        with jax.named_scope('pwait0'):
+            to_partner3(0).wait_recv()
+            recv3[0] = recv3[0] + part2
+            to_across(0).start()
+        for exp in range(n_exp):
+            tile_copy(exp, 2).start()
+
+    def first_chunk_near():
+        for exp in range(n_exp):
+            tile_copy(exp, 0).wait()
+        to_partner1(n_chunks - 1).wait_send()
+        with jax.named_scope('near_tiles'):
+            tile_rows(0, range(n_exp), (0, 1))
+        with jax.named_scope('near_combine'):
+            send1[...] = combine(1)
+            acc[0] = acc[0] + combine(0)
+            to_partner1(0).start()
 
     def chunk_step(j, first):
         for begin in range(0, n_exp, BATCH):
@@ -341,24 +383,22 @@
                 for exp in batch:
                     tile_copy(first + exp, j).wait()
             with jax.named_scope('tiles'):
-                for exp in batch:
-                    r = jnp.dot(h[pl.ds(exp * rows, rows), :], tile_place(first + exp)[...], preferred_element_type=F32).astype(BF16)
-                    for d in range(4):
-                        rbuf[d, pl.ds(exp * cap, cap), :] = r[d * cap:(d + 1) * cap]
-
-            @pl.when(j + 2 < n_chunks)
+                tile_rows(first, batch, range(4))
+
+            @pl.when((j + 2 < n_chunks) | (first == 0))
             def _():
                 for exp in batch:
-                    tile_copy(first + exp, j + 2).start()
+                    tile_copy(first + exp, lax.rem(j + 2, n_chunks)).start()
 
         @pl.when(j >= 3)
         def _():
             with jax.named_scope('su_wait'):
                 to_across(j - 3).wait_send()
 
-        @pl.when(j >= 1)
-        def _():
-            to_partner3(j - 1).wait_send()
+        to_partner3(j - 1).wait_send()
+
+        @pl.when(j >= 2)
+        def _():
             to_partner1(j - 1).wait_send()
 
         with jax.named_scope('combine3'):
@@ -374,29 +414,41 @@
             recv3[lax.rem(j, 4)] = recv3[lax.rem(j, 4)] + part2
             to_across(j).start()
 
-        @pl.when(j >= LAG)
+        @pl.when(j == LAG)
+        def _():
+            to_across(0).wait_recv()
+            acc[0] = acc[0] + recvu[0]
+
+        @pl.when(j > LAG)
         def _():
             with jax.named_scope('finish'):
                 finish(j - LAG)
 
     def two_chunks(i, carry):
-        chunk_step(2 * i, 0)
+        @pl.when(i == 0)
+        def _():
+            first_chunk()
+
+        @pl.when(i > 0)
+        def _():
+            chunk_step(2 * i, 0)
+
         chunk_step(2 * i + 1, n_exp)
         return carry
     lax.fori_loop(0, n_chunks // 2, two_chunks, 0)
 
-    def last_step(j, carry):
-        with jax.named_scope('last'):
-            finish(j)
-        return carry
-    lax.fori_loop(n_chunks - LAG, n_chunks, last_step, 0)
-
+    first_chunk_near()
     for copy in rt_copies + tok_across + tok_relay + [tok_partner]:
         copy.wait_send()
     to_partner3(n_chunks - 1).wait_send()
-    to_partner1(n_chunks - 1).wait_send()
-    for j in range(n_chunks - 3, n_chunks):
+    to_partner1(0).wait_recv()
+    y[:, pl.ds(0, CHUNK)] = (acc[0] + recv1[0]).astype(y.dtype)
+    to_partner1(0).wait_send()
+    to_across(n_chunks - 3).wait_send()
+    for j in range(n_chunks - LAG, n_chunks):
         to_across(j).wait_send()
+        with jax.named_scope('last'):
+            finish(j)
 
 
 def solution(mesh):
@@ -440,7 +492,7 @@
                 vm((n_chunks,) + block, F32),
                 vm(block, F32), vm(block, F32),
                 vm((4,) + block, F32), vm((4,) + block, F32), vm((6,) + block, F32),
-                dma((5,)), dma((RING, 2, n_blocks)), dma((n_blocks,)), dma((n_sub,)),
+                dma((PIECES + 4,)), dma((RING, 2, n_blocks)), dma((n_blocks,)), dma((n_sub,)),
                 dma((2 * PIECES + 1,)), dma((2 * PIECES + 1,)), dma((4,)), dma((4,)),
                 dma, dma, dma((n_chunks,)),
                 dma((n_chunks,)), dma((n_chunks,)), dma((n_chunks,)),

time: 133 us -> 132 us (level)
    pallas_call x1, Pallas kernels: 132 us -> 131 us  [device_step(): pl.pallas_call(functools.partial(moe_kernel, (n_tok, hidden, n_exp, ff, c...]
where the time goes in v5:
time: 132 us
  Pallas kernels  131 us (99%)
    pallas_call x1, Pallas kernels, device_step(): pl.pallas_call(functools.partial(moe_kernel, (n_tok, hidden, n_exp, ff, c...  131 us

profile of v5, /device:TPU:0, one launch (start us, length us, event | category | flops | bytes accessed | tf_op | source)
XLA Modules:
  0.0 131.6 jit_solution(6501081801352302812)
XLA Ops:
  0.0 130.6 %shard_map.109 = bf16[256,2048]{1,0:T(8,128)(2,1)S(1)} custom-call(bf16[256,2048]{1,0:T(8,128)(2,1)} %tok.1, s32[6,256]{1,0:T(8,128)} %bitcast.4, s32[6,256]{1,0:T(8,128)} %bitcast.5, f32[6,256]{1,0:T(8,128)} %bitcast.6, bf16[16,128]{1,0:T(8,128)(2,1)} %bitcast.7, bf16[2048,2816]{1,0:T(8,128)(2,1)} %sw1.1, bf16[2048,2816]{1,0:T(8,128)(2,1)} %sw3.1, ...), custom_call_target="tpu_custom_call" | custom-call | tf_op jit(solution)/shard_map/pallas_call | solution.py:475
  130.6 1.0 copy.13

commit v6 on v5

--- a/solution.py
+++ b/solution.py
@@ -17,6 +17,7 @@
 GROUP = 4
 BATCH = 8
 LAG = 2
+AHEAD = 1
 BF16_MAX = 3.3895313892515355e38
 
 
@@ -218,7 +219,7 @@
 
     with jax.named_scope('weights'):
         for d in range(4):
-            def weight_block(i, carry):
+            def weight_block(i):
                 row = (lax.broadcasted_iota(jnp.int32, (128, n_tok), 0) + i * 128).astype(F32) + base
                 g = jnp.zeros((128, n_tok), F32)
                 for k in range(top_k):
@@ -230,8 +231,12 @@
                 g3 = (left - g2.astype(F32)).astype(BF16)
                 for part, value in enumerate((g1, g2, g3)):
                     gs[d, :, pl.ds(pl.multiple_of(part * slots_all + i * 128, 128), 128)] = value
+
+            def weight_step(i, carry):
+                for u in range(3):
+                    weight_block(3 * i + u)
                 return carry
-            lax.fori_loop(0, slots_all // 128, weight_block, 0)
+            lax.fori_loop(0, slots_all // 384, weight_step, 0)
 
     def gather(g, sources):
         for d in sources:
@@ -246,9 +251,30 @@
                 for e in range(GROUP):
                     xg[pl.ds(e * rows + d * cap, cap), col] = got[e * cap:(e + 1) * cap]
 
+    def expert_rows(exp, slot, w1, begin=0, count=4 * cap):
+        x_rows = pl.ds(pl.multiple_of(lax.rem(exp, GROUP) * rows + begin, 16), count)
+        h_rows = exp * rows + begin
+        h_rows = pl.ds(h_rows if isinstance(exp, int) else pl.multiple_of(h_rows, 16), count)
+
+        def store_h(col, width, value):
+            h[h_rows, pl.ds(col, width)] = value
+
+        for b in range(n_blocks):
+            swiglu_block(lambda: xg[x_rows, :], w1, wbuf.at[slot, 1], b, store_h)
+
     with jax.named_scope('gather_near'):
         gather(jnp.int32(0), (0, 1))
     relay(PIECES // 2, PIECES - 2)
+
+    def ahead_step(exp, carry):
+        for b in range(n_blocks):
+            wait(expert_block(exp, b))
+        place = lax.rem(exp + 2, RING)
+        with jax.named_scope('ahead'):
+            expert_rows(exp, place, wbuf.at[place, 0], 0, rows // 2)
+        return carry
+    ahead_step(jnp.int32(0), 0)
+
 
     with jax.named_scope('dispatch_wait'):
         relay(PIECES - 2, PIECES)
@@ -256,9 +282,6 @@
         for copy in tok_relay:
             copy.wait_recv()
 
-    def h_rows(exp):
-        return pl.ds(exp * rows if isinstance(exp, int) else pl.multiple_of(exp * rows, rows), rows)
-
     def group_step(g, carry):
         with jax.named_scope('gather'):
             @pl.when(g == 0)
@@ -272,15 +295,6 @@
         def expert_step(i, carry):
             exp = g * GROUP + i
             place = lax.rem(exp + 2, RING)
-
-            def whole(e, slot, w1):
-                x_rows = pl.ds(pl.multiple_of(i * rows, rows), rows)
-
-                def store_h(col, width, value):
-                    h[h_rows(e), pl.ds(col, width)] = value
-
-                for b in range(n_blocks):
-                    swiglu_block(lambda: xg[x_rows, :], w1, wbuf.at[slot, 1], b, store_h)
 
             @pl.when(exp == RING)
             def _():
@@ -289,29 +303,29 @@
                         early_block(b).wait()
                         wait(expert_block(exp, b, (1,)))
                 with jax.named_scope('early'):
-                    whole(RING, (RING + 2) % RING, h.at[early_rows])
+                    expert_rows(RING, (RING + 2) % RING, h.at[early_rows])
                     for b in range(n_blocks):
                         start(expert_block(exp + RING, b, (1,)))
 
-            @pl.when(exp != RING)
+            @pl.when(exp < AHEAD)
+            def _():
+                with jax.named_scope('behind'):
+                    expert_rows(exp, place, wbuf.at[place, 0], rows // 2, rows // 2)
+
+                    for b in range(n_blocks):
+                        start(expert_block(exp + RING, b, (1,)))
+                    for b in range(n_blocks):
+                        start(expert_block(exp + 2 * RING, b, (0,)))
+
+            @pl.when((exp >= AHEAD) & (exp != RING))
             def _():
                 with jax.named_scope('w_wait'):
                     for b in range(n_blocks):
                         wait(expert_block(exp, b))
                 with jax.named_scope('expert'):
-                    whole(exp, place, wbuf.at[place, 0])
-
-                    @pl.when(exp == 0)
-                    def _():
-                        for b in range(n_blocks):
-                            start(expert_block(exp + RING, b, (1,)))
-                        for b in range(n_blocks):
-                            start(expert_block(exp + 2 * RING, b, (0,)))
-
-                    @pl.when(exp > 0)
-                    def _():
-                        for b in range(n_blocks):
-                            start_after(exp, b)
+                    expert_rows(exp, place, wbuf.at[place, 0])
+                    for b in range(n_blocks):
+                        start_after(exp, b)
             return carry
         lax.fori_loop(0, GROUP, expert_step, 0)
         return carry

time: 132 us -> 131 us (level)
  no operation moved by 1% of the time
where the time goes in v6:
time: 131 us
  Pallas kernels  130 us (99%)
    pallas_call x1, Pallas kernels, device_step(): pl.pallas_call(functools.partial(moe_kernel, (n_tok, hidden, n_exp, ff, c...  130 us

profile of v6, /device:TPU:0, one launch (start us, length us, event | category | flops | bytes accessed | tf_op | source)
XLA Modules:
  0.0 131.0 jit_solution(12776010959389658177)
XLA Ops:
  0.0 130.0 %shard_map.109 = bf16[256,2048]{1,0:T(8,128)(2,1)S(1)} custom-call(bf16[256,2048]{1,0:T(8,128)(2,1)} %tok.1, s32[6,256]{1,0:T(8,128)} %bitcast.4, s32[6,256]{1,0:T(8,128)} %bitcast.5, f32[6,256]{1,0:T(8,128)} %bitcast.6, bf16[16,128]{1,0:T(8,128)(2,1)} %bitcast.7, bf16[2048,2816]{1,0:T(8,128)(2,1)} %sw1.1, bf16[2048,2816]{1,0:T(8,128)(2,1)} %sw3.1, ...), custom_call_target="tpu_custom_call" | custom-call | tf_op jit(solution)/shard_map/pallas_call | solution.py:489
  130.0 1.0 copy.13

commit v7 on v6

--- a/solution.py
+++ b/solution.py
@@ -13,7 +13,7 @@
 CHUNK = 256
 BLOCK = 512
 RING = 3
-PIECES = 8
+PIECES = 16
 GROUP = 4
 BATCH = 8
 LAG = 2
@@ -264,7 +264,7 @@
 
     with jax.named_scope('gather_near'):
         gather(jnp.int32(0), (0, 1))
-    relay(PIECES // 2, PIECES - 2)
+    relay(PIECES // 2, PIECES - 4)
 
     def ahead_step(exp, carry):
         for b in range(n_blocks):
@@ -277,7 +277,7 @@
 
 
     with jax.named_scope('dispatch_wait'):
-        relay(PIECES - 2, PIECES)
+        relay(PIECES - 4, PIECES)
         gather(jnp.int32(0), (2,))
         for copy in tok_relay:
             copy.wait_recv()

time: 131 us -> 131 us (level)
  no operation moved by 1% of the time
where the time goes in v7:
time: 131 us
  Pallas kernels  130 us (99%)
    pallas_call x1, Pallas kernels, device_step(): pl.pallas_call(functools.partial(moe_kernel, (n_tok, hidden, n_exp, ff, c...  130 us

profile of v7, /device:TPU:0, one launch (start us, length us, event | category | flops | bytes accessed | tf_op | source)
XLA Modules:
  0.0 131.3 jit_solution(10088466254941374748)
XLA Ops:
  0.0 130.3 %shard_map.109 = bf16[256,2048]{1,0:T(8,128)(2,1)S(1)} custom-call(bf16[256,2048]{1,0:T(8,128)(2,1)} %tok.1, s32[6,256]{1,0:T(8,128)} %bitcast.4, s32[6,256]{1,0:T(8,128)} %bitcast.5, f32[6,256]{1,0:T(8,128)} %bitcast.6, bf16[16,128]{1,0:T(8,128)(2,1)} %bitcast.7, bf16[2048,2816]{1,0:T(8,128)(2,1)} %sw1.1, bf16[2048,2816]{1,0:T(8,128)(2,1)} %sw3.1, ...), custom_call_target="tpu_custom_call" | custom-call | tf_op jit(solution)/shard_map/pallas_call | solution.py:489
  130.3 1.0 copy.13
